TPU v7x, 32 devices: a whole 2x2x4 slice. The times are simulated.
32 devices in a mesh: dp: 16 (over z, y, core), rep: 2 (over x).
Axes of the slice: x: 2, y: 2, z: 4, core: 2. Of those that a mesh axis runs over, the one named last changes fastest.
Arguments:
- gate_pre: bfloat16 [2, 2048, 5632], P(None, 'dp', 'rep'), may hold values from -8 to 8
- up_pre: bfloat16 [2, 2048, 5632], P(None, 'dp', 'rep'), may hold values from -6 to 6
- out_grad: bfloat16 [2, 2048, 1024], P(None, 'dp'), may hold values from -6 to 6
- master: float32 [1024, 5632], P('dp', 'rep'), may hold values from -0.078125 to 0.078125
- moment_one: float32 [1024, 5632], P('dp', 'rep'), may hold values from -0.02 to 0.02
- moment_two: float32 [1024, 5632], P('dp', 'rep'), may hold values from 1e-06 to 1e-05
Outputs:
- layer_out: bfloat16 [2, 2048, 1024], P(None, 'dp', 'rep')
- gate_grad: bfloat16 [2, 2048, 5632], P(None, 'dp', 'rep')
- up_grad: bfloat16 [2, 2048, 5632], P(None, 'dp', 'rep')
- master_new: float32 [1024, 5632], P('dp', 'rep')
- moment_one_new: float32 [1024, 5632], P('dp', 'rep')
- moment_two_new: float32 [1024, 5632], P('dp', 'rep')
All inputs are finite; a program needn't handle non-finite values.
Results may differ from a plain program's by a relative error of at most 0.0048.
The roundings to bfloat16 on the way count: a program that leaves them out, or rounds other values in their place, can miss the bound.
Values may be sent and summed in bfloat16 or wider, within the bound.
A program may use at most 128 MiB of HBM per device.

v0:
```python
import functools

import jax
import jax.numpy as jnp
from jax import lax
from jax.experimental import pallas as pl
from jax.experimental.pallas import tpu as pltpu
from jax.sharding import PartitionSpec as P

first_power = 2.6561398887587544e-05
second_power = 0.005920529220333997

MESH = pl.DeviceIdType.MESH
CORES = 2
MID = 2


def adam(main_grad, master, moment_one, moment_two):
    first = 0.9 * moment_one + 0.1 * main_grad
    second = 0.95 * moment_two + 0.05 * main_grad * main_grad
    update = first / (1.0 - first_power) / (jnp.sqrt(second / (1.0 - second_power)) + 1e-08)
    return master - 0.003 * (update + 0.1 * master), first, second


def fused(
    outer, total,
    gate_hbm, up_hbm, cot_ref, master_ref, one_hbm, two_hbm,
    out_ref, gate_grad_ref, up_grad_ref, master_new_ref, first_ref, second_ref,
    weights, hid, hid_peer, cot_peer, own_sum, mid_send, mid_recv, outer_send, outer_recv,
    part_send, part_recv, cot_rows_ref, gate_ref, up_ref, one_ref, two_ref, local_sem,
    w_recv, w_mid_send, w_outer_send, w_core_send,
    core_send_sem, core_recv_sem,
    mid_send_sem, mid_recv_sem, outer_send_sem, outer_recv_sem, part_send_sem, part_recv_sem,
):
    me = lax.axis_index("dp")
    rep = lax.axis_index("rep")
    core = lax.rem(me, CORES)
    mid = lax.rem(me // CORES, MID)
    out = me // (CORES * MID)
    n = outer * MID * CORES
    rows, ff = master_ref.shape
    tokens = gate_ref.shape[0]
    loads = [
        pltpu.make_async_copy(src, dst, local_sem.at[index])
        for index, (src, dst) in enumerate(
            ((gate_hbm, gate_ref), (up_hbm, up_ref), (one_hbm, one_ref), (two_hbm, two_ref))
        )
    ]
    for load in loads:
        load.start()
    width = 256 if ff % 256 == 0 else 128
    chunks = ff // width

    def at(o, m, c):
        return (o * MID + m) * CORES + c

    core_peer = {"dp": at(out, mid, 1 - core)}
    mid_peer = {"dp": at(out, 1 - mid, core)}
    rep_peer = {"rep": 1 - rep}

    def outer_at(k):
        return lax.rem(out + k, outer)

    def outer_peer(k):
        return {"dp": at(outer_at(k), mid, core)}

    def remote(src, dst, send, recv, device):
        return pltpu.make_async_remote_copy(
            src_ref=src, dst_ref=dst, send_sem=send, recv_sem=recv,
            device_id=device, device_id_type=MESH,
        )

    weights[me] = master_ref[...].astype(jnp.bfloat16)
    barrier = pltpu.get_barrier_semaphore()
    peers = [core_peer, mid_peer, rep_peer] + [outer_peer(k) for k in range(1, outer)]
    for peer in peers:
        pl.semaphore_signal(barrier, inc=1, device_id=peer, device_id_type=MESH)
    pl.semaphore_wait(barrier, len(peers))

    order = sorted(range(1, outer), key=lambda k: min(k, outer - k))
    started = []

    def go(copy):
        copy.start()
        started.append(copy)
        return copy

    for k in order:
        go(remote(weights.at[me], weights.at[me], w_outer_send.at[k], w_recv.at[me], outer_peer(k)))
    go(remote(weights.at[me], weights.at[me], w_mid_send.at[0], w_recv.at[me], mid_peer))
    go(remote(weights.at[me], weights.at[me], w_core_send.at[0], w_recv.at[me], core_peer))
    turned = jnp.transpose(cot_ref[...].astype(jnp.float32)).astype(jnp.bfloat16).reshape(n, rows, tokens)
    for o in range(outer):
        for m in range(MID):
            for c in range(CORES):
                cot_rows_ref[c, m, o] = turned[at(o, m, c)]
    loads[0].wait()
    loads[1].wait()

    def columns(j):
        return pl.ds(pl.multiple_of(j * width, width), width)

    def hidden_step(j, carry):
        cols = columns(j)
        gate = gate_ref[:, cols].astype(jnp.float32)
        sig = jax.nn.sigmoid(gate)
        hid[:, cols] = (gate * sig * up_ref[:, cols].astype(jnp.float32)).astype(jnp.bfloat16)
        return carry

    lax.fori_loop(0, chunks, hidden_step, 0)
    cot_copy = go(remote(cot_rows_ref.at[1 - core], cot_peer, core_send_sem.at[0], core_recv_sem.at[0], core_peer))
    hid_copy = go(remote(hid, hid_peer, core_send_sem.at[1], core_recv_sem.at[1], core_peer))
    cot_copy.wait_recv()
    hid_copy.wait_recv()

    def grad_of(which, cols):
        own = cot_rows_ref[core, which].reshape(outer * rows, tokens)
        other = cot_peer[which].reshape(outer * rows, tokens)
        value = jnp.dot(own, hid[:, cols], preferred_element_type=jnp.float32)
        value += jnp.dot(other, hid_peer[:, cols], preferred_element_type=jnp.float32)
        return value.reshape(outer, rows, width)

    def send_step(j, carry):
        cols = columns(j)
        mid_send[:, :, cols] = grad_of(1 - mid, cols).astype(jnp.bfloat16)
        return carry

    lax.fori_loop(0, chunks, send_step, 0)

    def reduce_mid(k):
        slot = outer_at(k)
        go(remote(mid_send.at[slot], mid_recv.at[slot], mid_send_sem.at[k], mid_recv_sem.at[slot], mid_peer))

    def arrival(slot):
        return remote(weights.at[slot], weights.at[slot], w_core_send.at[0], w_recv.at[slot], core_peer)

    def forward_outer(k):
        slot = at(lax.rem(out + outer - k, outer), mid, core)
        arrival(slot).wait_recv()
        go(remote(weights.at[slot], weights.at[slot], w_mid_send.at[k], w_recv.at[slot], mid_peer))
        go(remote(weights.at[slot], weights.at[slot], w_core_send.at[k], w_recv.at[slot], core_peer))

    def forward_mid(k):
        slot = at(lax.rem(out + outer - k, outer), 1 - mid, core)
        arrival(slot).wait_recv()
        go(remote(weights.at[slot], weights.at[slot], w_core_send.at[outer + k], w_recv.at[slot], core_peer))

    def mid_wait(slot):
        remote(mid_recv.at[slot], mid_recv.at[slot], mid_send_sem.at[0], mid_recv_sem.at[slot], mid_peer).wait_recv()

    def pass_on(k):
        slot = outer_at(k)
        mid_wait(slot)

        def step(j, carry):
            cols = columns(j)
            outer_send[slot, :, cols] = (
                own_sum[slot, :, cols] + mid_recv[slot, :, cols].astype(jnp.float32)
            ).astype(jnp.bfloat16)
            return carry

        lax.fori_loop(0, chunks, step, 0)
        go(remote(outer_send.at[slot], outer_recv.at[out], outer_send_sem.at[k], outer_recv_sem.at[out], outer_peer(k)))

    back = list(reversed(order))
    forward_outer(order[0])
    reduce_mid(back[0])
    def own_step(j, carry):
        cols = columns(j)
        own_sum[:, :, cols] = grad_of(mid, cols)
        return carry

    lax.fori_loop(0, chunks, own_step, 0)

    forward_mid(0)
    for index in range(1, outer - 1):
        forward_outer(order[index])
        reduce_mid(back[index])
        if index < outer - 2:
            pass_on(back[index - 1])
    reduce_mid(0)
    for k in order[:-1]:
        forward_mid(k)
    if outer > 2:
        pass_on(back[-2])
    forward_mid(order[-1])
    for k in range(outer):
        for m in range(MID):
            arrival(at(outer_at(k), m, 1 - core)).wait_recv()

    half = n // 2
    group = max(1, min(half, 256 // rows))

    def part_step(base, target):
        def step(g, carry):
            some = weights[pl.ds(base + g * group, group)].reshape(group * rows, ff)
            target[g] = lax.dot_general(
                hid[...], some, (((1,), (1,)), ((), ())), preferred_element_type=jnp.float32
            )
            return carry

        lax.fori_loop(0, half // group, step, 0)

    part_step((1 - rep) * half, part_send)
    part_copy = go(remote(part_send, part_recv, part_send_sem, part_recv_sem, rep_peer))

    def input_step(j, carry):
        cols = columns(j)
        grad = jnp.dot(
            cot_ref[...], weights[:, :, cols].reshape(n * rows, width),
            preferred_element_type=jnp.float32,
        )
        gate = gate_ref[:, cols].astype(jnp.float32)
        up_val = up_ref[:, cols].astype(jnp.float32)
        sig = jax.nn.sigmoid(gate)
        gate_grad_ref[:, cols] = (grad * up_val * sig * (1.0 + gate * (1.0 - sig))).astype(jnp.bfloat16)
        up_grad_ref[:, cols] = (grad * gate * sig).astype(jnp.bfloat16)
        return carry

    lax.fori_loop(0, chunks // 2, input_step, 0)
    pass_on(back[-1])
    lax.fori_loop(chunks // 2, chunks, input_step, 0)

    part_copy.wait_recv()
    base = rep * half
    for g in range(half // group):
        some = weights[pl.ds(base + g * group, group)].reshape(group * rows, ff)
        own = lax.dot_general(
            hid[...], some, (((1,), (1,)), ((), ())), preferred_element_type=jnp.float32
        )
        out_ref[:, g * group * rows : (g + 1) * group * rows] = (own + part_recv[g]).astype(jnp.bfloat16)

    mid_wait(out)
    sources = [lax.rem(out + outer - k, outer) for k in range(1, outer)]
    for source in sources:
        remote(outer_recv.at[source], outer_recv.at[source], outer_send_sem.at[0], outer_recv_sem.at[source], mid_peer).wait_recv()

    loads[2].wait()
    loads[3].wait()

    def update_step(j, carry):
        cols = columns(j)
        grad = own_sum[out, :, cols] + mid_recv[out, :, cols].astype(jnp.float32)
        for source in sources:
            grad += outer_recv[source, :, cols].astype(jnp.float32)
        master_new, first, second = adam(
            grad / jnp.float32(total), master_ref[:, cols], one_ref[:, cols], two_ref[:, cols]
        )
        master_new_ref[:, cols] = master_new
        first_ref[:, cols] = first
        second_ref[:, cols] = second
        return carry

    lax.fori_loop(0, chunks, update_step, 0)
    for copy in started:
        copy.wait_send()


def handed_on(values):
    steps = 4

    def body(*refs):
        for source, target in zip(refs[: len(values)], refs[len(values) :]):
            target[...] = source[...]

    specs = [
        pl.BlockSpec((value.shape[0] // steps, value.shape[1]), lambda i: (i, 0)) for value in values
    ]
    return pl.pallas_call(
        body,
        grid=(steps,),
        out_shape=[jax.ShapeDtypeStruct(value.shape, value.dtype) for value in values],
        in_specs=specs,
        out_specs=specs,
    )(*values)


def in_one_kernel(size, gate_pre, up_pre, out_grad, master, moment_one, moment_two):
    micro, count, ff = gate_pre.shape
    tokens, depth, rows = micro * count, out_grad.shape[2], master.shape[0]
    outer = size // (MID * CORES)
    half = size // 2
    group = max(1, min(half, 256 // rows))
    cot = out_grad.reshape(tokens, depth)
    vmem = pl.BlockSpec(memory_space=pltpu.VMEM)
    hbm = pl.BlockSpec(memory_space=pl.ANY)
    bf, f32 = jnp.bfloat16, jnp.float32
    dma = pltpu.SemaphoreType.DMA
    results = pl.pallas_call(
        functools.partial(fused, outer, tokens * size),
        out_shape=(
            jax.ShapeDtypeStruct((tokens, depth // 2), bf),
            jax.ShapeDtypeStruct((tokens, ff), bf),
            jax.ShapeDtypeStruct((tokens, ff), bf),
            jax.ShapeDtypeStruct((rows, ff), f32),
            jax.ShapeDtypeStruct((rows, ff), f32),
            jax.ShapeDtypeStruct((rows, ff), f32),
        ),
        in_specs=[hbm, hbm, vmem, vmem, hbm, hbm],
        out_specs=(vmem,) * 6,
        scratch_shapes=[
            pltpu.VMEM((size, rows, ff), bf),
            pltpu.VMEM((tokens, ff), bf),
            pltpu.VMEM((tokens, ff), bf),
            pltpu.VMEM((MID, outer, rows, tokens), bf),
            pltpu.VMEM((outer, rows, ff), f32),
            pltpu.VMEM((outer, rows, ff), bf),
            pltpu.VMEM((outer, rows, ff), bf),
            pltpu.VMEM((outer, rows, ff), bf),
            pltpu.VMEM((outer, rows, ff), bf),
            pltpu.VMEM((half // group, tokens, group * rows), f32),
            pltpu.VMEM((half // group, tokens, group * rows), f32),
            pltpu.VMEM((CORES, MID, outer, rows, tokens), bf),
            pltpu.VMEM((tokens, ff), bf),
            pltpu.VMEM((tokens, ff), bf),
            pltpu.VMEM((rows, ff), f32),
            pltpu.VMEM((rows, ff), f32),
            dma((4,)),
            dma((size,)), dma((outer,)), dma((outer,)), dma((2 * outer,)),
            dma((2,)), dma((2,)),
            dma((outer,)), dma((outer,)), dma((outer,)), dma((outer,)), dma, dma,
        ],
        compiler_params=pltpu.CompilerParams(
            collective_id=0, has_side_effects=True, vmem_limit_bytes=60 * 1024 * 1024
        ),
    )(
        gate_pre.reshape(tokens, ff), up_pre.reshape(tokens, ff), cot, master, moment_one, moment_two,
    )
    results = handed_on(results)
    split = [value.reshape(micro, count, value.shape[1]) for value in results[:3]]
    return (*split, *results[3:])


def with_collectives(gate_pre, up_pre, out_grad, master, moment_one, moment_two):
    weights = lax.all_gather(master.astype(jnp.bfloat16), "dp", axis=0, tiled=True)
    micro = gate_pre.shape[0]
    total = micro * gate_pre.shape[1] * lax.axis_size("dp")
    outs_list = []
    gate_list = []
    up_list = []
    grad_sum = None
    for index in range(micro):
        gate = gate_pre[index].astype(jnp.float32)
        up_val = up_pre[index].astype(jnp.float32)
        sig = jax.nn.sigmoid(gate)
        hidden = (gate * sig * up_val).astype(jnp.bfloat16)
        partial_out = lax.dot_general(
            hidden, weights, (((1,), (1,)), ((), ())), preferred_element_type=jnp.float32
        )
        outs_list.append(
            lax.psum_scatter(partial_out, "rep", scatter_dimension=1, tiled=True).astype(
                jnp.bfloat16
            )
        )
        hid_grad = jnp.dot(out_grad[index], weights, preferred_element_type=jnp.float32)
        gate_list.append(
            (hid_grad * up_val * sig * (1.0 + gate * (1.0 - sig))).astype(jnp.bfloat16)
        )
        up_list.append((hid_grad * gate * sig).astype(jnp.bfloat16))
        term = lax.dot_general(
            out_grad[index], hidden, (((0,), (0,)), ((), ())), preferred_element_type=jnp.float32
        )
        shard = lax.psum_scatter(term, "dp", scatter_dimension=0, tiled=True)
        grad_sum = shard if grad_sum is None else grad_sum + shard
    updated = adam(grad_sum / jnp.float32(total), master, moment_one, moment_two)
    return jnp.stack(outs_list), jnp.stack(gate_list), jnp.stack(up_list), *updated


def solution(mesh):
    size = mesh.shape["dp"]

    def on_device(gate_pre, up_pre, out_grad, master, moment_one, moment_two):
        tall = master.shape[0] % 16 == 0 and size % (MID * CORES) == 0 and size > MID * CORES
        step = functools.partial(in_one_kernel, size) if tall else with_collectives
        return step(gate_pre, up_pre, out_grad, master, moment_one, moment_two)

    split = P(None, "dp", "rep")
    owned = P("dp", "rep")
    return jax.shard_map(
        on_device,
        mesh=mesh,
        in_specs=(split, split, P(None, "dp", None), owned, owned, owned),
        out_specs=(split, split, split, owned, owned, owned),
        check_vma=False,
    )
```

profile of v0, /device:TPU:17, one launch (start us, length us, event | category | flops | bytes accessed | tf_op | source)
XLA Modules:
  0.0 87.3 jit_solution(17245487683676542665)
XLA Ops:
  0.6 81.4 %shard_map.109 = (bf16[256,512]{1,0:T(8,128)(2,1)}, bf16[256,2816]{1,0:T(8,128)(2,1)}, bf16[256,2816]{1,0:T(8,128)(2,1)}, f32[64,2816]{1,0:T(8,128)}, f32[64,2816]{1,0:T(8,128)}, /*index=5*/f32[64,2816]{1,0:T(8,128)}) custom-call(bf16[256,2816]{1,0:T(8,128)(2,1)} %bitcast.6, bf16[256,2816]{1,0:T(8,128)(2,1)} %bitcast.7, bf16[256,1024]{1,0:T(8,128)(2,1)} %bitcast.8, ...), custom_call_target="tpu_custom_call" | custom-call | tf_op jit(solution)/shard_map/pallas_call | solution.py:289
  82.0 5.3 %shard_map.110 = (bf16[256,512]{1,0:T(8,128)(2,1)}, bf16[256,2816]{1,0:T(8,128)(2,1)}, bf16[256,2816]{1,0:T(8,128)(2,1)}, f32[64,2816]{1,0:T(8,128)}, f32[64,2816]{1,0:T(8,128)}, /*index=5*/f32[64,2816]{1,0:T(8,128)}) custom-call(bf16[256,512]{1,0:T(8,128)(2,1)} %get-tuple-element.18.refs_0_, bf16[256,2816]{1,0:T(8,128)(2,1)} %get-tuple-element.19.refs_1_, ...), custom_call_target="tpu_custom_call" | custom-call | tf_op jit(solution)/shard_map/pallas_call | solution.py:269
where the time goes:
time: 87.5 us; the launch traced here: 87.3 us
  Pallas kernels  86.7 us (99%)
    pallas_call x1, Pallas kernels, in_one_kernel(): pl.pallas_call(functools.partial(fused, outer, tokens * size), out_shape=...  81.4 us
    pallas_call x1, Pallas kernels, handed_on(): pl.pallas_call(body, grid=(steps,), out_shape=[jax.ShapeDtypeStruct(value...  5.29 us

commit v1 on v0

--- a/solution.py
+++ b/solution.py
@@ -257,22 +257,26 @@
 
 
 def handed_on(values):
-    steps = 4
+    count = len(values)
 
     def body(*refs):
-        for source, target in zip(refs[: len(values)], refs[len(values) :]):
-            target[...] = source[...]
-
-    specs = [
-        pl.BlockSpec((value.shape[0] // steps, value.shape[1]), lambda i: (i, 0)) for value in values
-    ]
+        sems = refs[-1]
+        copies = [
+            pltpu.make_async_copy(refs[index], refs[count + index], sems.at[index]) for index in range(count)
+        ]
+        for copy in copies:
+            copy.start()
+        for copy in copies:
+            copy.wait()
+
     return pl.pallas_call(
         body,
-        grid=(steps,),
         out_shape=[jax.ShapeDtypeStruct(value.shape, value.dtype) for value in values],
-        in_specs=specs,
-        out_specs=specs,
-    )(*values)
+        in_specs=[pl.BlockSpec(memory_space=pltpu.VMEM)] * count,
+        out_specs=[pl.BlockSpec(memory_space=pl.ANY)] * count,
+        scratch_shapes=[pltpu.SemaphoreType.DMA((count,))],
+        compiler_params=pltpu.CompilerParams(vmem_limit_bytes=8 * 1024 * 1024),
+    )(*[pltpu.with_memory_space_constraint(value, pltpu.VMEM) for value in values])
 
 
 def in_one_kernel(size, gate_pre, up_pre, out_grad, master, moment_one, moment_two):
@@ -289,12 +293,12 @@
     results = pl.pallas_call(
         functools.partial(fused, outer, tokens * size),
         out_shape=(
-            jax.ShapeDtypeStruct((tokens, depth // 2), bf),
-            jax.ShapeDtypeStruct((tokens, ff), bf),
-            jax.ShapeDtypeStruct((tokens, ff), bf),
-            jax.ShapeDtypeStruct((rows, ff), f32),
-            jax.ShapeDtypeStruct((rows, ff), f32),
-            jax.ShapeDtypeStruct((rows, ff), f32),
+            pltpu.VMEM((tokens, depth // 2), bf),
+            pltpu.VMEM((tokens, ff), bf),
+            pltpu.VMEM((tokens, ff), bf),
+            pltpu.VMEM((rows, ff), f32),
+            pltpu.VMEM((rows, ff), f32),
+            pltpu.VMEM((rows, ff), f32),
         ),
         in_specs=[hbm, hbm, vmem, vmem, hbm, hbm],
         out_specs=(vmem,) * 6,
@@ -321,7 +325,7 @@
             dma((outer,)), dma((outer,)), dma((outer,)), dma((outer,)), dma, dma,
         ],
         compiler_params=pltpu.CompilerParams(
-            collective_id=0, has_side_effects=True, vmem_limit_bytes=60 * 1024 * 1024
+            collective_id=0, has_side_effects=True, vmem_limit_bytes=50 * 1024 * 1024
         ),
     )(
         gate_pre.reshape(tokens, ff), up_pre.reshape(tokens, ff), cot, master, moment_one, moment_two,

time: 87.5 us -> 82.3 us (0.941)
  Pallas kernels: 86.7 us -> 81.5 us
    pallas_call x1, Pallas kernels: 5.29 us -> 2.42 us  [handed_on(): pl.pallas_call(body, out_shape=[jax.ShapeDtypeStruct(value.shape, value.d...]
    pallas_call x1, Pallas kernels: 81.4 us -> 79.1 us  [in_one_kernel(): pl.pallas_call(functools.partial(fused, outer, tokens * size), out_shape=...]
where the time goes in v1:
time: 82.3 us; the launch traced here: 82.1 us
  Pallas kernels  81.5 us (99%)
    pallas_call x1, Pallas kernels, in_one_kernel(): pl.pallas_call(functools.partial(fused, outer, tokens * size), out_shape=...  79.1 us
    pallas_call x1, Pallas kernels, handed_on(): pl.pallas_call(body, out_shape=[jax.ShapeDtypeStruct(value.shape, value.d...  2.42 us

profile of v1, /device:TPU:17, one launch (start us, length us, event | category | flops | bytes accessed | tf_op | source)
XLA Modules:
  0.0 82.1 jit_solution(9767985446575053388)
XLA Ops:
  0.6 79.1 %shard_map.109 = (bf16[256,512]{1,0:T(8,128)(2,1)S(1)}, bf16[256,2816]{1,0:T(8,128)(2,1)S(1)}, bf16[256,2816]{1,0:T(8,128)(2,1)S(1)}, f32[64,2816]{1,0:T(8,128)S...) custom-call(bf16[256,2816]{1,0:T(8,128)(2,1)} %bitcast.6, bf16[256,2816]{1,0:T(8,128)(2,1)} %bitcast.7, ...), custom_call_target="tpu_custom_call" | custom-call | tf_op jit(solution)/shard_map/pallas_call | solution.py:293
  79.7 2.4 %shard_map.110 = (bf16[256,512]{1,0:T(8,128)(2,1)}, bf16[256,2816]{1,0:T(8,128)(2,1)}, bf16[256,2816]{1,0:T(8,128)(2,1)}, f32[64,2816]{1,0:T(8,128)}, f32[64,2816]{1,0:T(8,128)}, /*index=5*/f32[64,2816]{1,0:T(8,128)}) custom-call(bf16[256,512]{1,0:T(8,128)(2,1)S(1)} %get-tuple-element.18.refs_0_, bf16[256,2816]{1,0:T(8,128)(2,1)S(1)} %get-tuple-element.19.refs_1_, ...), custom_call_target="tpu_custom_call" | custom-call | tf_op jit(solution)/shard_map/pallas_call | solution.py:272

commit v2 on v1

v2 whole, which is shorter than its diff:
```python
import functools

import jax
import jax.numpy as jnp
from jax import lax
from jax.experimental import pallas as pl
from jax.experimental.pallas import tpu as pltpu
from jax.sharding import PartitionSpec as P

first_power = 2.6561398887587544e-05
second_power = 0.005920529220333997

MESH = pl.DeviceIdType.MESH
CORES = 2
MID = 2
WIDTH = 256
ALONG = 0.32


def adam(main_grad, master, moment_one, moment_two):
    first = 0.9 * moment_one + 0.1 * main_grad
    second = 0.95 * moment_two + 0.05 * main_grad * main_grad
    update = first / (1.0 - first_power) / (jnp.sqrt(second / (1.0 - second_power)) + 1e-08)
    return master - 0.003 * (update + 0.1 * master), first, second


def fused(
    outer, total, split,
    gate_hbm, up_hbm, cot_hbm, master_hbm, one_hbm, two_hbm,
    out_ref, gate_grad_ref, up_grad_ref, master_new_ref, first_ref, second_ref,
    weights, hid, hid_peer, cot_peer, own_sum, mid_send, mid_recv, line_send, line_recv,
    part, part_send, part_recv, hid_grad, cot_rows_ref,
    gate_ref, up_ref, cot_ref, master_ref, one_ref, two_ref,
    local_sem, send_sem, w_recv, core_recv, mid_recv_sem, line_recv_sem, part_recv_sem,
):
    me = lax.axis_index("dp")
    rep = lax.axis_index("rep")
    core = lax.rem(me, CORES)
    mid = lax.rem(me // CORES, MID)
    out = me // (CORES * MID)
    n = outer * MID * CORES
    block = MID * CORES
    rows, ff = master_ref.shape
    tokens = gate_ref.shape[0]
    loads = [
        pltpu.make_async_copy(src, dst, local_sem.at[index])
        for index, (src, dst) in enumerate(
            (
                (master_hbm, master_ref), (gate_hbm, gate_ref), (up_hbm, up_ref), (cot_hbm, cot_ref),
                (one_hbm, one_ref), (two_hbm, two_ref),
            )
        )
    ]
    for load in loads:
        load.start()
    width = WIDTH
    chunks = ff // width
    lead = (chunks + 1) // 2
    pieces = (pl.ds(0, lead * width), pl.ds(lead * width, ff - lead * width))
    parts = (pl.ds(0, split), pl.ds(split, ff - split))
    last = outer - 1
    low = out < outer // 2

    def at(o, m, c):
        return (o * MID + m) * CORES + c

    core_peer = {"dp": at(out, mid, 1 - core)}
    mid_peer = {"dp": at(out, 1 - mid, core)}
    rep_peer = {"rep": 1 - rep}
    next_peer = {"dp": at(jnp.minimum(out + 1, last), mid, core)}
    prev_peer = {"dp": at(jnp.maximum(out - 1, 0), mid, core)}
    has_next = out < last
    has_prev = out > 0

    def remote(src, dst, send, recv, device):
        return pltpu.make_async_remote_copy(
            src_ref=src, dst_ref=dst, send_sem=send, recv_sem=recv,
            device_id=device, device_id_type=MESH,
        )

    started = []

    def go(ends, device, cond=None, inside=None):
        index = len(started)

        def make():
            src, dst, recv = ends()
            return remote(src, dst, send_sem.at[index], recv, device)

        if cond is None:
            make().start()
        else:
            pl.when(cond)(lambda: make().start())
        started.append((make, [given for given in (inside, cond) if given is not None]))

    barrier = pltpu.get_barrier_semaphore()
    for peer in (core_peer, mid_peer, rep_peer):
        pl.semaphore_signal(barrier, inc=1, device_id=peer, device_id_type=MESH)

    @pl.when(has_next)
    def _():
        pl.semaphore_signal(barrier, inc=1, device_id=next_peer, device_id_type=MESH)

    @pl.when(has_prev)
    def _():
        pl.semaphore_signal(barrier, inc=1, device_id=prev_peer, device_id_type=MESH)

    loads[0].wait()
    weights[me] = master_ref[...].astype(jnp.bfloat16)
    pl.semaphore_wait(barrier, 3 + has_next.astype(jnp.int32) + has_prev.astype(jnp.int32))

    def w_go(slot, which, device, cond=None, inside=None):
        def ends():
            ref = weights.at[slot, :, parts[which]]
            return ref, ref, w_recv.at[which, slot]

        go(ends, device, cond, inside)

    def w_wait(slot, which):
        ref = weights.at[slot, :, parts[which]]
        remote(ref, ref, send_sem.at[0], w_recv.at[which, slot], core_peer).wait_recv()

    w_go(me, 1, mid_peer)
    w_go(me, 0, next_peer, has_next)
    w_go(me, 0, prev_peer, has_prev)
    w_go(me, 1, next_peer, has_next)
    w_go(me, 1, prev_peer, has_prev)
    w_go(me, 0, mid_peer)
    w_go(me, 1, core_peer)
    w_go(me, 0, core_peer)

    def along(k, m, which):
        for cond, slot, device, more in (
            (out >= k, at(out - k, m, core), next_peer, has_next),
            (out + k <= last, at(out + k, m, core), prev_peer, has_prev),
        ):
            @pl.when(cond)
            def _():
                w_wait(slot, which)
                w_go(slot, which, device, more, cond)
                if which == 0:
                    w_go(slot, which, mid_peer, None, cond)
                w_go(slot, which, core_peer, None, cond)

    def across_first():
        slot = at(out, 1 - mid, core)
        w_wait(slot, 1)
        w_go(slot, 1, next_peer, has_next)
        w_go(slot, 1, prev_peer, has_prev)
        w_go(slot, 1, core_peer)

    def across_last(k):
        sides = ((out >= k, out - k), (out + k <= last, out + k))
        for cond, o in sides if k else sides[:1]:
            slot = at(o, 1 - mid, core)

            @pl.when(cond)
            def _():
                w_wait(slot, 0)
                w_go(slot, 0, core_peer, None, cond)

    loads[3].wait()
    turned = jnp.transpose(cot_ref[...].astype(jnp.float32)).astype(jnp.bfloat16).reshape(n, rows, tokens)
    for o in range(outer):
        for m in range(MID):
            for c in range(CORES):
                cot_rows_ref[c, m, o] = turned[at(o, m, c)]
    go(lambda: (cot_rows_ref.at[1 - core], cot_peer, core_recv.at[0]), core_peer)
    loads[1].wait()
    loads[2].wait()

    def columns(j):
        return pl.ds(pl.multiple_of(j * width, width), width)

    def hidden_step(j, carry):
        cols = columns(j)
        gate = gate_ref[:, cols].astype(jnp.float32)
        sig = jax.nn.sigmoid(gate)
        hid[:, cols] = (gate * sig * up_ref[:, cols].astype(jnp.float32)).astype(jnp.bfloat16)
        return carry

    bounds = ((0, lead), (lead, chunks))
    for p, (lo, hi) in enumerate(bounds):
        lax.fori_loop(lo, hi, hidden_step, 0)
        go(
            lambda p=p: (hid.at[:, pieces[p]], hid_peer.at[:, pieces[p]], core_recv.at[1 + p]),
            core_peer,
        )

    def core_wait(p):
        ref = hid_peer.at[:, pieces[p]]
        remote(ref, ref, send_sem.at[0], core_recv.at[1 + p], core_peer).wait_recv()

    def grad_of(which, cols):
        own = cot_rows_ref[core, which].reshape(outer * rows, tokens)
        other = cot_peer[which].reshape(outer * rows, tokens)
        value = jnp.dot(own, hid[:, cols], preferred_element_type=jnp.float32)
        value += jnp.dot(other, hid_peer[:, cols], preferred_element_type=jnp.float32)
        return value.reshape(outer, rows, width)

    def send_step(j, carry):
        cols = columns(j)
        mid_send[:, :, cols] = grad_of(1 - mid, cols).astype(jnp.bfloat16)
        return carry

    def own_step(j, carry):
        cols = columns(j)
        own_sum[:, :, cols] = grad_of(mid, cols)
        return carry

    def target(i):
        if i == last:
            return out
        down = last - i
        down = jnp.where(down <= out, down - 1, down)
        return jnp.where(low, down, jnp.where(i >= out, i + 1, i))

    def reduce_across(i):
        t = target(i)
        for h in range(2):
            go(
                lambda h=h: (
                    mid_send.at[t, :, pieces[h]], mid_recv.at[t, :, pieces[h]], mid_recv_sem.at[h, t],
                ),
                mid_peer,
            )

    def mid_wait(t, h):
        ref = mid_recv.at[t, :, pieces[h]]
        remote(ref, ref, send_sem.at[0], mid_recv_sem.at[h, t], mid_peer).wait_recv()

    def line_wait(d, t, h):
        ref = line_recv.at[d, t, :, pieces[h]]
        remote(ref, ref, send_sem.at[0], line_recv_sem.at[d, h, t], mid_peer).wait_recv()

    def pass_on(i, h, cond=None):
        t = target(i)
        d = jnp.where(t > out, 0, 1)
        more = jnp.where(t > out, has_prev, has_next)
        lo, hi = bounds[h]
        toward = {"dp": at(out + 1 - 2 * d, mid, core)}

        def step(chained):
            def inner(j, carry):
                cols = columns(j)
                value = own_sum[t, :, cols] + mid_recv[t, :, cols].astype(jnp.float32)
                if chained:
                    value += line_recv[d, t, :, cols].astype(jnp.float32)
                line_send[t, :, cols] = value.astype(jnp.bfloat16)
                return carry

            return inner

        def run():
            mid_wait(t, h)

            @pl.when(more)
            def _():
                line_wait(d, t, h)
                lax.fori_loop(lo, hi, step(True), 0)

            @pl.when(jnp.logical_not(more))
            def _():
                lax.fori_loop(lo, hi, step(False), 0)

            go(
                lambda: (
                    line_send.at[t, :, pieces[h]], line_recv.at[d, t, :, pieces[h]],
                    line_recv_sem.at[d, h, t],
                ),
                toward, None, cond,
            )

        if cond is None:
            run()
        else:
            pl.when(cond)(run)

    def nearest(j):
        if j == 0:
            return out
        k = (j + 1) // 2
        z = jnp.where(low, out, last - out)
        g = jnp.where(j <= 2 * z, z - k if j % 2 else z + k, j)
        return jnp.where(low, g, last - g)

    half = outer // 2
    deep = block * rows

    def use_block(j):
        g = nearest(j)
        for m in range(MID):
            for which in range(2):
                w_wait(at(g, m, 1 - core), which)
        some = weights[pl.ds(g * block, block)].reshape(deep, ff)
        value = lax.dot_general(hid[...], some, (((1,), (1,)), ((), ())), preferred_element_type=jnp.float32)
        part[g] = value
        part_send[g] = value.astype(jnp.bfloat16)
        place = lax.rem(g, half)
        go(
            lambda: (part_send.at[g], part_recv.at[place], part_recv_sem.at[place]),
            rep_peer, g // half != rep,
        )
        cot = cot_ref[:, pl.ds(pl.multiple_of(g * deep, deep), deep)]

        def step(i, carry):
            cols = columns(i)
            grad = jnp.dot(
                cot, weights[pl.ds(g * block, block), :, cols].reshape(deep, width),
                preferred_element_type=jnp.float32,
            )
            if j > 0:
                grad += hid_grad[:, cols]
            if j < last:
                hid_grad[:, cols] = grad
            else:
                gate = gate_ref[:, cols].astype(jnp.float32)
                up_val = up_ref[:, cols].astype(jnp.float32)
                sig = jax.nn.sigmoid(gate)
                gate_grad_ref[:, cols] = (grad * up_val * sig * (1.0 + gate * (1.0 - sig))).astype(jnp.bfloat16)
                up_grad_ref[:, cols] = (grad * gate * sig).astype(jnp.bfloat16)
            return carry

        lax.fori_loop(0, chunks, step, 0)

    edge = jnp.logical_or(out == 0, out == last)
    inner = jnp.logical_not(edge)
    along(1, mid, 0)
    for p, (lo, hi) in enumerate(bounds):
        if p == 0:
            ref = cot_peer
            remote(ref, ref, send_sem.at[0], core_recv.at[0], core_peer).wait_recv()
        core_wait(p)
        lax.fori_loop(lo, hi, send_step, 0)
        if p == 0:
            across_first()
    reduce_across(0)
    across_last(0)
    lax.fori_loop(0, chunks, own_step, 0)
    along(1, mid, 1)
    if outer > 2:
        along(2, mid, 0)
    reduce_across(1)
    use_block(0)
    across_last(1)
    along(1, 1 - mid, 1)
    pass_on(0, 0, edge)
    pass_on(0, 1, edge)
    use_block(1)
    for k in range(2, outer):
        across_last(k)
        if k == 2:
            pass_on(0, 0, inner)
        along(k, mid, 1)
        if k == 2:
            pass_on(0, 1, inner)
        if k < last:
            along(k + 1, mid, 0)
            reduce_across(k)
        if k == last - 1:
            reduce_across(last)
        pass_on(k - 1, 0)
        along(k, 1 - mid, 1)
        pass_on(k - 1, 1)
        use_block(k)
    loads[4].wait()
    loads[5].wait()

    @pl.when(jnp.logical_not(has_prev))
    def _():
        line_recv[0, out] = jnp.zeros((rows, ff), jnp.bfloat16)

    @pl.when(jnp.logical_not(has_next))
    def _():
        line_recv[1, out] = jnp.zeros((rows, ff), jnp.bfloat16)

    def update_step(j, carry):
        cols = columns(j)
        grad = own_sum[out, :, cols] + mid_recv[out, :, cols].astype(jnp.float32)
        grad += line_recv[0, out, :, cols].astype(jnp.float32) + line_recv[1, out, :, cols].astype(jnp.float32)
        master_new, first, second = adam(
            grad / jnp.float32(total), master_ref[:, cols], one_ref[:, cols], two_ref[:, cols]
        )
        master_new_ref[:, cols] = master_new
        first_ref[:, cols] = first
        second_ref[:, cols] = second
        return carry

    for h, (lo, hi) in enumerate(bounds):
        pl.when(has_prev)(lambda: line_wait(0, out, h))
        pl.when(has_next)(lambda: line_wait(1, out, h))
        mid_wait(out, h)
        lax.fori_loop(lo, hi, update_step, 0)

    for place in range(half):
        ref = part_recv.at[place]
        remote(ref, ref, send_sem.at[0], part_recv_sem.at[place], rep_peer).wait_recv()
        out_ref[:, place * deep : (place + 1) * deep] = (
            part[rep * half + place] + part_recv[place].astype(jnp.float32)
        ).astype(jnp.bfloat16)
    for make, given in started:
        if given:
            pl.when(functools.reduce(jnp.logical_and, given))(lambda: make().wait_send())
        else:
            make().wait_send()


def handed_on(values):
    count = len(values)

    def body(*refs):
        sems = refs[-1]
        copies = [
            pltpu.make_async_copy(refs[index], refs[count + index], sems.at[index]) for index in range(count)
        ]
        for copy in copies:
            copy.start()
        for copy in copies:
            copy.wait()

    return pl.pallas_call(
        body,
        out_shape=[jax.ShapeDtypeStruct(value.shape, value.dtype) for value in values],
        in_specs=[pl.BlockSpec(memory_space=pltpu.VMEM)] * count,
        out_specs=[pl.BlockSpec(memory_space=pl.ANY)] * count,
        scratch_shapes=[pltpu.SemaphoreType.DMA((count,))],
        compiler_params=pltpu.CompilerParams(vmem_limit_bytes=8 * 1024 * 1024),
    )(*[pltpu.with_memory_space_constraint(value, pltpu.VMEM) for value in values])


def in_one_kernel(size, gate_pre, up_pre, out_grad, master, moment_one, moment_two):
    micro, count, ff = gate_pre.shape
    tokens, depth, rows = micro * count, out_grad.shape[2], master.shape[0]
    outer = size // (MID * CORES)
    deep = MID * CORES * rows
    split = max(1, round(ff * ALONG / 128)) * 128
    cot = out_grad.reshape(tokens, depth)
    hbm = pl.BlockSpec(memory_space=pl.ANY)
    bf, f32 = jnp.bfloat16, jnp.float32
    dma = pltpu.SemaphoreType.DMA
    results = pl.pallas_call(
        functools.partial(fused, outer, tokens * size, split),
        out_shape=(
            pltpu.VMEM((tokens, depth // 2), bf),
            pltpu.VMEM((tokens, ff), bf),
            pltpu.VMEM((tokens, ff), bf),
            pltpu.VMEM((rows, ff), f32),
            pltpu.VMEM((rows, ff), f32),
            pltpu.VMEM((rows, ff), f32),
        ),
        in_specs=[hbm] * 6,
        out_specs=(pl.BlockSpec(memory_space=pltpu.VMEM),) * 6,
        scratch_shapes=[
            pltpu.VMEM((size, rows, ff), bf),
            pltpu.VMEM((tokens, ff), bf),
            pltpu.VMEM((tokens, ff), bf),
            pltpu.VMEM((MID, outer, rows, tokens), bf),
            pltpu.VMEM((outer, rows, ff), f32),
            pltpu.VMEM((outer, rows, ff), bf),
            pltpu.VMEM((outer, rows, ff), bf),
            pltpu.VMEM((outer, rows, ff), bf),
            pltpu.VMEM((2, outer, rows, ff), bf),
            pltpu.VMEM((outer, tokens, deep), f32),
            pltpu.VMEM((outer, tokens, deep), bf),
            pltpu.VMEM((outer // 2, tokens, deep), bf),
            pltpu.VMEM((tokens, ff), f32),
            pltpu.VMEM((CORES, MID, outer, rows, tokens), bf),
            pltpu.VMEM((tokens, ff), bf),
            pltpu.VMEM((tokens, ff), bf),
            pltpu.VMEM((tokens, depth), bf),
            pltpu.VMEM((rows, ff), f32),
            pltpu.VMEM((rows, ff), f32),
            pltpu.VMEM((rows, ff), f32),
            dma((6,)), dma((40 * outer,)), dma((2, size)), dma((3,)),
            dma((2, outer)), dma((2, 2, outer)), dma((outer // 2,)),
        ],
        compiler_params=pltpu.CompilerParams(
            collective_id=0, has_side_effects=True, vmem_limit_bytes=50 * 1024 * 1024
        ),
    )(
        gate_pre.reshape(tokens, ff), up_pre.reshape(tokens, ff), cot, master, moment_one, moment_two,
    )
    results = handed_on(results)
    split = [value.reshape(micro, count, value.shape[1]) for value in results[:3]]
    return (*split, *results[3:])


def with_collectives(gate_pre, up_pre, out_grad, master, moment_one, moment_two):
    weights = lax.all_gather(master.astype(jnp.bfloat16), "dp", axis=0, tiled=True)
    micro = gate_pre.shape[0]
    total = micro * gate_pre.shape[1] * lax.axis_size("dp")
    outs_list = []
    gate_list = []
    up_list = []
    grad_sum = None
    for index in range(micro):
        gate = gate_pre[index].astype(jnp.float32)
        up_val = up_pre[index].astype(jnp.float32)
        sig = jax.nn.sigmoid(gate)
        hidden = (gate * sig * up_val).astype(jnp.bfloat16)
        partial_out = lax.dot_general(
            hidden, weights, (((1,), (1,)), ((), ())), preferred_element_type=jnp.float32
        )
        outs_list.append(
            lax.psum_scatter(partial_out, "rep", scatter_dimension=1, tiled=True).astype(
                jnp.bfloat16
            )
        )
        hid_grad = jnp.dot(out_grad[index], weights, preferred_element_type=jnp.float32)
        gate_list.append(
            (hid_grad * up_val * sig * (1.0 + gate * (1.0 - sig))).astype(jnp.bfloat16)
        )
        up_list.append((hid_grad * gate * sig).astype(jnp.bfloat16))
        term = lax.dot_general(
            out_grad[index], hidden, (((0,), (0,)), ((), ())), preferred_element_type=jnp.float32
        )
        shard = lax.psum_scatter(term, "dp", scatter_dimension=0, tiled=True)
        grad_sum = shard if grad_sum is None else grad_sum + shard
    updated = adam(grad_sum / jnp.float32(total), master, moment_one, moment_two)
    return jnp.stack(outs_list), jnp.stack(gate_list), jnp.stack(up_list), *updated


def solution(mesh):
    size = mesh.shape["dp"]

    def on_device(gate_pre, up_pre, out_grad, master, moment_one, moment_two):
        tall = master.shape[0] % 32 == 0 and master.shape[1] % WIDTH == 0 and size % (2 * MID * CORES) == 0
        step = functools.partial(in_one_kernel, size) if tall else with_collectives
        return step(gate_pre, up_pre, out_grad, master, moment_one, moment_two)

    split = P(None, "dp", "rep")
    owned = P("dp", "rep")
    return jax.shard_map(
        on_device,
        mesh=mesh,
        in_specs=(split, split, P(None, "dp", None), owned, owned, owned),
        out_specs=(split, split, split, owned, owned, owned),
        check_vma=False,
    )
```

time: 82.3 us -> 57.6 us (0.70)
  the two profiles are of different devices: /device:TPU:17 before, /device:TPU:0 now
where the time goes in v2:
time: 57.6 us; the launch traced here: 57.5 us
  Pallas kernels  56.8 us (99%)
  between operations  0.64 us (1%)
    pallas_call x1, Pallas kernels, in_one_kernel(): pl.pallas_call(functools.partial(fused, outer, tokens * size, split), out...  54.4 us
    pallas_call x1, Pallas kernels, handed_on(): pl.pallas_call(body, out_shape=[jax.ShapeDtypeStruct(value.shape, value.d...  2.42 us

profile of v2, /device:TPU:0, one launch (start us, length us, event | category | flops | bytes accessed | tf_op | source)
XLA Modules:
  0.0 57.5 jit_solution(14653154214429917561)
XLA Ops:
  0.6 54.4 %shard_map.109 = (bf16[256,512]{1,0:T(8,128)(2,1)S(1)}, bf16[256,2816]{1,0:T(8,128)(2,1)S(1)}, bf16[256,2816]{1,0:T(8,128)(2,1)S(1)}, f32[64,2816]{1,0:T(8,128)S...) custom-call(bf16[256,2816]{1,0:T(8,128)(2,1)} %bitcast.6, bf16[256,2816]{1,0:T(8,128)(2,1)} %bitcast.7, ...), custom_call_target="tpu_custom_call" | custom-call | tf_op jit(solution)/shard_map/pallas_call | solution.py:441
  55.0 2.4 %shard_map.110 = (bf16[256,512]{1,0:T(8,128)(2,1)}, bf16[256,2816]{1,0:T(8,128)(2,1)}, bf16[256,2816]{1,0:T(8,128)(2,1)}, f32[64,2816]{1,0:T(8,128)}, f32[64,2816]{1,0:T(8,128)}, /*index=5*/f32[64,2816]{1,0:T(8,128)}) custom-call(bf16[256,512]{1,0:T(8,128)(2,1)S(1)} %get-tuple-element.18.refs_0_, bf16[256,2816]{1,0:T(8,128)(2,1)S(1)} %get-tuple-element.19.refs_1_, ...), custom_call_target="tpu_custom_call" | custom-call | tf_op jit(solution)/shard_map/pallas_call | solution.py:421

commit v3 on v2

--- a/solution.py
+++ b/solution.py
@@ -14,7 +14,8 @@
 CORES = 2
 MID = 2
 WIDTH = 256
-ALONG = 0.32
+ALONG = 0.6
+ACROSS = 0.636
 
 
 def adam(main_grad, master, moment_one, moment_two):
@@ -25,13 +26,14 @@
 
 
 def fused(
-    outer, total, split,
+    outer, total, split, early,
     gate_hbm, up_hbm, cot_hbm, master_hbm, one_hbm, two_hbm,
     out_ref, gate_grad_ref, up_grad_ref, master_new_ref, first_ref, second_ref,
     weights, hid, hid_peer, cot_peer, own_sum, mid_send, mid_recv, line_send, line_recv,
+    wide_sum, wide_send, wide_recv, cross_send, cross_recv,
     part, part_send, part_recv, hid_grad, cot_rows_ref,
     gate_ref, up_ref, cot_ref, master_ref, one_ref, two_ref,
-    local_sem, send_sem, w_recv, core_recv, mid_recv_sem, line_recv_sem, part_recv_sem,
+    local_sem, send_sem, w_recv, core_recv, mid_recv_sem, line_recv_sem, wide_recv_sem, cross_recv_sem, part_recv_sem,
 ):
     me = lax.axis_index("dp")
     rep = lax.axis_index("rep")
@@ -55,8 +57,12 @@
         load.start()
     width = WIDTH
     chunks = ff // width
-    lead = (chunks + 1) // 2
-    pieces = (pl.ds(0, lead * width), pl.ds(lead * width, ff - lead * width))
+    first = early // width
+    lead = (first + 1) // 2
+    bounds = ((0, lead), (lead, first))
+    pieces = (pl.ds(0, lead * width), pl.ds(lead * width, early - lead * width))
+    sides = ((first, chunks), (0, first))
+    halves = (pl.ds(early, ff - early), pl.ds(0, early))
     parts = (pl.ds(0, split), pl.ds(split, ff - split))
     last = outer - 1
     low = out < outer // 2
@@ -179,16 +185,15 @@
         hid[:, cols] = (gate * sig * up_ref[:, cols].astype(jnp.float32)).astype(jnp.bfloat16)
         return carry
 
-    bounds = ((0, lead), (lead, chunks))
-    for p, (lo, hi) in enumerate(bounds):
+    for p, (lo, hi) in enumerate(sides):
         lax.fori_loop(lo, hi, hidden_step, 0)
         go(
-            lambda p=p: (hid.at[:, pieces[p]], hid_peer.at[:, pieces[p]], core_recv.at[1 + p]),
+            lambda p=p: (hid.at[:, halves[p]], hid_peer.at[:, halves[p]], core_recv.at[1 + p]),
             core_peer,
         )
 
     def core_wait(p):
-        ref = hid_peer.at[:, pieces[p]]
+        ref = hid_peer.at[:, halves[p]]
         remote(ref, ref, send_sem.at[0], core_recv.at[1 + p], core_peer).wait_recv()
 
     def grad_of(which, cols):
@@ -201,6 +206,14 @@
     def send_step(j, carry):
         cols = columns(j)
         mid_send[:, :, cols] = grad_of(1 - mid, cols).astype(jnp.bfloat16)
+        return carry
+
+    def wide_columns(j):
+        return pl.ds(pl.multiple_of(j * width - early, width), width)
+
+    def wide_step(j, carry):
+        for m in range(MID):
+            wide_sum[m, :, :, wide_columns(j)] = grad_of(m, columns(j))
         return carry
 
     def own_step(j, carry):
@@ -275,6 +288,78 @@
             run()
         else:
             pl.when(cond)(run)
+
+    def wide_wait(d, m, t):
+        ref = wide_recv.at[d, m, t]
+        remote(ref, ref, send_sem.at[0], wide_recv_sem.at[d, m, t], mid_peer).wait_recv()
+
+    def wide_on(i, p, cond=None):
+        t = target(i)
+        m = mid if p else 1 - mid
+        d = jnp.where(t > out, 0, 1)
+        more = jnp.where(t > out, has_prev, has_next)
+        toward = {"dp": at(out + 1 - 2 * d, mid, core)}
+
+        def step(chained):
+            def inner(j, carry):
+                cols = wide_columns(j)
+                value = wide_sum[m, t, :, cols]
+                if chained:
+                    value += wide_recv[d, m, t, :, cols].astype(jnp.float32)
+                wide_send[m, t, :, cols] = value.astype(jnp.bfloat16)
+                return carry
+
+            return inner
+
+        def run():
+            @pl.when(more)
+            def _():
+                wide_wait(d, m, t)
+                lax.fori_loop(first, chunks, step(True), 0)
+
+            @pl.when(jnp.logical_not(more))
+            def _():
+                lax.fori_loop(first, chunks, step(False), 0)
+
+            go(
+                lambda: (wide_send.at[m, t], wide_recv.at[d, m, t], wide_recv_sem.at[d, m, t]),
+                toward, None, cond,
+            )
+
+        if cond is None:
+            run()
+        else:
+            pl.when(cond)(run)
+
+    def wide_total(m, cols):
+        value = wide_sum[m, out, :, cols]
+        value += wide_recv[0, m, out, :, cols].astype(jnp.float32)
+        return value + wide_recv[1, m, out, :, cols].astype(jnp.float32)
+
+    def wide_arrived(m):
+        pl.when(has_prev)(lambda: wide_wait(0, m, out))
+        pl.when(has_next)(lambda: wide_wait(1, m, out))
+
+    def wide_across():
+        wide_arrived(1 - mid)
+
+        def step(j, carry):
+            cols = wide_columns(j)
+            cross_send[:, cols] = wide_total(1 - mid, cols).astype(jnp.bfloat16)
+            return carry
+
+        lax.fori_loop(first, chunks, step, 0)
+        go(lambda: (cross_send, cross_recv, cross_recv_sem), mid_peer)
+
+    @pl.when(jnp.logical_not(has_prev))
+    def _():
+        line_recv[0, out] = jnp.zeros((rows, early), jnp.bfloat16)
+        wide_recv[0, :, out] = jnp.zeros((MID, rows, ff - early), jnp.bfloat16)
+
+    @pl.when(jnp.logical_not(has_next))
+    def _():
+        line_recv[1, out] = jnp.zeros((rows, early), jnp.bfloat16)
+        wide_recv[1, :, out] = jnp.zeros((MID, rows, ff - early), jnp.bfloat16)
 
     def nearest(j):
         if j == 0:
@@ -325,72 +410,103 @@
 
     edge = jnp.logical_or(out == 0, out == last)
     inner = jnp.logical_not(edge)
+    ref = cot_peer
+    remote(ref, ref, send_sem.at[0], core_recv.at[0], core_peer).wait_recv()
+    core_wait(0)
+    lax.fori_loop(first, chunks, wide_step, 0)
+    for p in range(MID):
+        wide_on(0, p, edge)
+    across_first()
     along(1, mid, 0)
-    for p, (lo, hi) in enumerate(bounds):
-        if p == 0:
-            ref = cot_peer
-            remote(ref, ref, send_sem.at[0], core_recv.at[0], core_peer).wait_recv()
-        core_wait(p)
-        lax.fori_loop(lo, hi, send_step, 0)
-        if p == 0:
-            across_first()
+    core_wait(1)
+    lax.fori_loop(0, first, send_step, 0)
     reduce_across(0)
+    lax.fori_loop(0, first, own_step, 0)
+    along(1, mid, 1)
+    if last > 1:
+        for p in range(MID):
+            wide_on(1, p, edge)
     across_last(0)
-    lax.fori_loop(0, chunks, own_step, 0)
-    along(1, mid, 1)
-    if outer > 2:
+    along(1, 1 - mid, 1)
+    use_block(0)
+    across_last(1)
+    wide_on(0, 0, inner)
+    pass_on(0, 0, edge)
+    if last > 1:
         along(2, mid, 0)
     reduce_across(1)
-    use_block(0)
-    across_last(1)
-    along(1, 1 - mid, 1)
-    pass_on(0, 0, edge)
+    wide_on(0, 1, inner)
     pass_on(0, 1, edge)
-    use_block(1)
+    if last > 1:
+        use_block(1)
     for k in range(2, outer):
-        across_last(k)
+        along(k, mid, 1)
+        if k == 2:
+            wide_on(1, 0, inner)
+        along(k, 1 - mid, 1)
+        if k == 2:
+            wide_on(1, 1, inner)
+        if k < last:
+            for p in range(MID):
+                wide_on(k, p, edge)
         if k == 2:
             pass_on(0, 0, inner)
-        along(k, mid, 1)
-        if k == 2:
-            pass_on(0, 1, inner)
         if k < last:
             along(k + 1, mid, 0)
             reduce_across(k)
         if k == last - 1:
             reduce_across(last)
-        pass_on(k - 1, 0)
-        along(k, 1 - mid, 1)
-        pass_on(k - 1, 1)
-        use_block(k)
+        if k == 2:
+            pass_on(0, 1, inner)
+        if k < last:
+            for p in range(MID):
+                wide_on(k, p, inner)
+        across_last(k)
+        if k < last:
+            pass_on(k - 1, 0, edge)
+            pass_on(k - 1, 1, edge)
+            use_block(k)
+    for h in range(2):
+        for k in range(last - 1, 0, -1):
+            pass_on(k, h, inner)
+    wide_across()
+    if last > 1:
+        pass_on(last - 1, 0, edge)
+        pass_on(last - 1, 1, edge)
+    use_block(last)
     loads[4].wait()
     loads[5].wait()
 
-    @pl.when(jnp.logical_not(has_prev))
-    def _():
-        line_recv[0, out] = jnp.zeros((rows, ff), jnp.bfloat16)
-
-    @pl.when(jnp.logical_not(has_next))
-    def _():
-        line_recv[1, out] = jnp.zeros((rows, ff), jnp.bfloat16)
-
-    def update_step(j, carry):
+    def update_step(total_of):
+        def step(j, carry):
+            cols = columns(j)
+            master_new, moment, square = adam(
+                total_of(j) / jnp.float32(total), master_ref[:, cols], one_ref[:, cols], two_ref[:, cols]
+            )
+            master_new_ref[:, cols] = master_new
+            first_ref[:, cols] = moment
+            second_ref[:, cols] = square
+            return carry
+
+        return step
+
+    def early_total(j):
         cols = columns(j)
-        grad = own_sum[out, :, cols] + mid_recv[out, :, cols].astype(jnp.float32)
-        grad += line_recv[0, out, :, cols].astype(jnp.float32) + line_recv[1, out, :, cols].astype(jnp.float32)
-        master_new, first, second = adam(
-            grad / jnp.float32(total), master_ref[:, cols], one_ref[:, cols], two_ref[:, cols]
-        )
-        master_new_ref[:, cols] = master_new
-        first_ref[:, cols] = first
-        second_ref[:, cols] = second
-        return carry
+        value = own_sum[out, :, cols] + mid_recv[out, :, cols].astype(jnp.float32)
+        return value + line_recv[0, out, :, cols].astype(jnp.float32) + line_recv[1, out, :, cols].astype(jnp.float32)
+
+    def late_total(j):
+        cols = wide_columns(j)
+        return wide_total(mid, cols) + cross_recv[:, cols].astype(jnp.float32)
 
     for h, (lo, hi) in enumerate(bounds):
         pl.when(has_prev)(lambda: line_wait(0, out, h))
         pl.when(has_next)(lambda: line_wait(1, out, h))
         mid_wait(out, h)
-        lax.fori_loop(lo, hi, update_step, 0)
+        lax.fori_loop(lo, hi, update_step(early_total), 0)
+    wide_arrived(mid)
+    remote(cross_recv, cross_recv, send_sem.at[0], cross_recv_sem, mid_peer).wait_recv()
+    lax.fori_loop(first, chunks, update_step(late_total), 0)
 
     for place in range(half):
         ref = part_recv.at[place]
@@ -434,12 +550,13 @@
     outer = size // (MID * CORES)
     deep = MID * CORES * rows
     split = max(1, round(ff * ALONG / 128)) * 128
+    early = max(1, round(ff * ACROSS / WIDTH)) * WIDTH
     cot = out_grad.reshape(tokens, depth)
     hbm = pl.BlockSpec(memory_space=pl.ANY)
     bf, f32 = jnp.bfloat16, jnp.float32
     dma = pltpu.SemaphoreType.DMA
     results = pl.pallas_call(
-        functools.partial(fused, outer, tokens * size, split),
+        functools.partial(fused, outer, tokens * size, split, early),
         out_shape=(
             pltpu.VMEM((tokens, depth // 2), bf),
             pltpu.VMEM((tokens, ff), bf),
@@ -455,11 +572,16 @@
             pltpu.VMEM((tokens, ff), bf),
             pltpu.VMEM((tokens, ff), bf),
             pltpu.VMEM((MID, outer, rows, tokens), bf),
-            pltpu.VMEM((outer, rows, ff), f32),
-            pltpu.VMEM((outer, rows, ff), bf),
-            pltpu.VMEM((outer, rows, ff), bf),
-            pltpu.VMEM((outer, rows, ff), bf),
-            pltpu.VMEM((2, outer, rows, ff), bf),
+            pltpu.VMEM((outer, rows, early), f32),
+            pltpu.VMEM((outer, rows, early), bf),
+            pltpu.VMEM((outer, rows, early), bf),
+            pltpu.VMEM((outer, rows, early), bf),
+            pltpu.VMEM((2, outer, rows, early), bf),
+            pltpu.VMEM((MID, outer, rows, ff - early), f32),
+            pltpu.VMEM((MID, outer, rows, ff - early), bf),
+            pltpu.VMEM((2, MID, outer, rows, ff - early), bf),
+            pltpu.VMEM((rows, ff - early), bf),
+            pltpu.VMEM((rows, ff - early), bf),
             pltpu.VMEM((outer, tokens, deep), f32),
             pltpu.VMEM((outer, tokens, deep), bf),
             pltpu.VMEM((outer // 2, tokens, deep), bf),
@@ -472,7 +594,7 @@
             pltpu.VMEM((rows, ff), f32),
             pltpu.VMEM((rows, ff), f32),
             dma((6,)), dma((40 * outer,)), dma((2, size)), dma((3,)),
-            dma((2, outer)), dma((2, 2, outer)), dma((outer // 2,)),
+            dma((2, outer)), dma((2, 2, outer)), dma((2, MID, outer)), dma, dma((outer // 2,)),
         ],
         compiler_params=pltpu.CompilerParams(
             collective_id=0, has_side_effects=True, vmem_limit_bytes=50 * 1024 * 1024
@@ -524,7 +646,7 @@
     size = mesh.shape["dp"]
 
     def on_device(gate_pre, up_pre, out_grad, master, moment_one, moment_two):
-        tall = master.shape[0] % 32 == 0 and master.shape[1] % WIDTH == 0 and size % (2 * MID * CORES) == 0
+        tall = master.shape[0] % 32 == 0 and master.shape[1] % WIDTH == 0 and size in (2 * MID * CORES, 4 * MID * CORES)
         step = functools.partial(in_one_kernel, size) if tall else with_collectives
         return step(gate_pre, up_pre, out_grad, master, moment_one, moment_two)
 

time: 57.6 us -> 55.9 us (0.970)
  Pallas kernels: 56.8 us -> 55.1 us
    pallas_call x1, Pallas kernels: 54.4 us -> 52.7 us  [in_one_kernel(): pl.pallas_call(functools.partial(fused, outer, tokens * size, split, earl...]
where the time goes in v3:
time: 55.9 us; the launch traced here: 55.8 us
  Pallas kernels  55.1 us (99%)
  between operations  0.64 us (1%)
    pallas_call x1, Pallas kernels, in_one_kernel(): pl.pallas_call(functools.partial(fused, outer, tokens * size, split, earl...  52.7 us
    pallas_call x1, Pallas kernels, handed_on(): pl.pallas_call(body, out_shape=[jax.ShapeDtypeStruct(value.shape, value.d...  2.42 us

profile of v3, /device:TPU:0, one launch (start us, length us, event | category | flops | bytes accessed | tf_op | source)
XLA Modules:
  0.0 55.8 jit_solution(12897916005049695513)
XLA Ops:
  0.6 52.7 %shard_map.109 = (bf16[256,512]{1,0:T(8,128)(2,1)S(1)}, bf16[256,2816]{1,0:T(8,128)(2,1)S(1)}, bf16[256,2816]{1,0:T(8,128)(2,1)S(1)}, f32[64,2816]{1,0:T(8,128)S...) custom-call(bf16[256,2816]{1,0:T(8,128)(2,1)} %bitcast.6, bf16[256,2816]{1,0:T(8,128)(2,1)} %bitcast.7, ...), custom_call_target="tpu_custom_call" | custom-call | tf_op jit(solution)/shard_map/pallas_call | solution.py:558
  53.3 2.4 %shard_map.110 = (bf16[256,512]{1,0:T(8,128)(2,1)}, bf16[256,2816]{1,0:T(8,128)(2,1)}, bf16[256,2816]{1,0:T(8,128)(2,1)}, f32[64,2816]{1,0:T(8,128)}, f32[64,2816]{1,0:T(8,128)}, /*index=5*/f32[64,2816]{1,0:T(8,128)}) custom-call(bf16[256,512]{1,0:T(8,128)(2,1)S(1)} %get-tuple-element.18.refs_0_, bf16[256,2816]{1,0:T(8,128)(2,1)S(1)} %get-tuple-element.19.refs_1_, ...), custom_call_target="tpu_custom_call" | custom-call | tf_op jit(solution)/shard_map/pallas_call | solution.py:537

commit v4 on v3

--- a/solution.py
+++ b/solution.py
@@ -13,9 +13,25 @@
 MESH = pl.DeviceIdType.MESH
 CORES = 2
 MID = 2
+LINE = 4
+LANES = 128
 WIDTH = 256
-ALONG = 0.6
-ACROSS = 0.636
+BROAD = 1408
+ALONG = 0.591
+ACROSS = 0.591
+LEAD = 0.462
+ORDER = (
+    ("first",), ("core", 0), ("core", 1), ("along", 1, 0, 0), ("wide",), ("wedge", 0, 0), ("send",),
+    ("across", 1, 0), ("wedge", 0, 1), ("last", 0), ("across", 0, 0), ("block", 0), ("along", 1, 0, 1),
+    ("across", 0, 1), ("across", 1, 1), ("wedge", 1, 0), ("winner", 0, 0), ("wedge", 2, 0),
+    ("along", 1, 1, 1), ("own",), ("along", 2, 0, 0), ("edge", 0, 1), ("winner", 0, 1), ("edge", 1, 1),
+    ("winner", 2, 0), ("across", 2, 1), ("edge", 0, 0), ("last", 1), ("wedge", 1, 1), ("winner", 1, 0),
+    ("inner", 0, 1), ("across", 2, 0), ("along", 2, 0, 1), ("edge", 1, 0), ("block", 1), ("along", 2, 1, 1),
+    ("wedge", 2, 1), ("along", 3, 0, 0), ("across", 3, 1), ("inner", 1, 1), ("winner", 2, 1), ("last", 2),
+    ("inner", 0, 0), ("edge", 2, 1), ("cross",), ("block", 2), ("edge", 2, 0), ("across", 3, 0),
+    ("along", 3, 0, 1), ("along", 3, 1, 1), ("last", 3), ("winner", 1, 1), ("inner", 2, 1), ("block", 3),
+    ("inner", 2, 0), ("inner", 1, 0), ("fin", 1), ("finw",), ("fin", 0),
+)
 
 
 def adam(main_grad, master, moment_one, moment_two):
@@ -44,6 +60,59 @@
     block = MID * CORES
     rows, ff = master_ref.shape
     tokens = gate_ref.shape[0]
+    lead = max(1, round(early * LEAD / LANES)) * LANES
+    bounds = ((0, lead), (lead, early))
+    pieces = tuple(pl.ds(lo, hi - lo) for lo, hi in bounds)
+    sides = ((early, ff), (0, early))
+    halves = tuple(pl.ds(lo, hi - lo) for lo, hi in sides)
+    parts = (pl.ds(0, split), pl.ds(split, ff - split))
+    last = outer - 1
+    low = out < outer // 2
+
+    def at(o, m, c):
+        return (o * MID + m) * CORES + c
+
+    core_peer = {"dp": at(out, mid, 1 - core)}
+    mid_peer = {"dp": at(out, 1 - mid, core)}
+    rep_peer = {"rep": 1 - rep}
+    next_peer = {"dp": at(jnp.minimum(out + 1, last), mid, core)}
+    prev_peer = {"dp": at(jnp.maximum(out - 1, 0), mid, core)}
+    has_next = out < last
+    has_prev = out > 0
+
+    def remote(src, dst, send, recv, device):
+        return pltpu.make_async_remote_copy(
+            src_ref=src, dst_ref=dst, send_sem=send, recv_sem=recv,
+            device_id=device, device_id_type=MESH,
+        )
+
+    started = []
+
+    def go(ends, device, cond=None, inside=None):
+        index = len(started)
+
+        def make():
+            src, dst, recv = ends()
+            return remote(src, dst, send_sem.at[index], recv, device)
+
+        if cond is None:
+            make().start()
+        else:
+            pl.when(cond)(lambda: make().start())
+        started.append((make, [given for given in (inside, cond) if given is not None]))
+
+    barrier = pltpu.get_barrier_semaphore()
+    for peer in (core_peer, mid_peer, rep_peer):
+        pl.semaphore_signal(barrier, inc=1, device_id=peer, device_id_type=MESH)
+
+    @pl.when(has_next)
+    def _():
+        pl.semaphore_signal(barrier, inc=1, device_id=next_peer, device_id_type=MESH)
+
+    @pl.when(has_prev)
+    def _():
+        pl.semaphore_signal(barrier, inc=1, device_id=prev_peer, device_id_type=MESH)
+
     loads = [
         pltpu.make_async_copy(src, dst, local_sem.at[index])
         for index, (src, dst) in enumerate(
@@ -55,62 +124,6 @@
     ]
     for load in loads:
         load.start()
-    width = WIDTH
-    chunks = ff // width
-    first = early // width
-    lead = (first + 1) // 2
-    bounds = ((0, lead), (lead, first))
-    pieces = (pl.ds(0, lead * width), pl.ds(lead * width, early - lead * width))
-    sides = ((first, chunks), (0, first))
-    halves = (pl.ds(early, ff - early), pl.ds(0, early))
-    parts = (pl.ds(0, split), pl.ds(split, ff - split))
-    last = outer - 1
-    low = out < outer // 2
-
-    def at(o, m, c):
-        return (o * MID + m) * CORES + c
-
-    core_peer = {"dp": at(out, mid, 1 - core)}
-    mid_peer = {"dp": at(out, 1 - mid, core)}
-    rep_peer = {"rep": 1 - rep}
-    next_peer = {"dp": at(jnp.minimum(out + 1, last), mid, core)}
-    prev_peer = {"dp": at(jnp.maximum(out - 1, 0), mid, core)}
-    has_next = out < last
-    has_prev = out > 0
-
-    def remote(src, dst, send, recv, device):
-        return pltpu.make_async_remote_copy(
-            src_ref=src, dst_ref=dst, send_sem=send, recv_sem=recv,
-            device_id=device, device_id_type=MESH,
-        )
-
-    started = []
-
-    def go(ends, device, cond=None, inside=None):
-        index = len(started)
-
-        def make():
-            src, dst, recv = ends()
-            return remote(src, dst, send_sem.at[index], recv, device)
-
-        if cond is None:
-            make().start()
-        else:
-            pl.when(cond)(lambda: make().start())
-        started.append((make, [given for given in (inside, cond) if given is not None]))
-
-    barrier = pltpu.get_barrier_semaphore()
-    for peer in (core_peer, mid_peer, rep_peer):
-        pl.semaphore_signal(barrier, inc=1, device_id=peer, device_id_type=MESH)
-
-    @pl.when(has_next)
-    def _():
-        pl.semaphore_signal(barrier, inc=1, device_id=next_peer, device_id_type=MESH)
-
-    @pl.when(has_prev)
-    def _():
-        pl.semaphore_signal(barrier, inc=1, device_id=prev_peer, device_id_type=MESH)
-
     loads[0].wait()
     weights[me] = master_ref[...].astype(jnp.bfloat16)
     pl.semaphore_wait(barrier, 3 + has_next.astype(jnp.int32) + has_prev.astype(jnp.int32))
@@ -175,18 +188,28 @@
     loads[1].wait()
     loads[2].wait()
 
-    def columns(j):
-        return pl.ds(pl.multiple_of(j * width, width), width)
-
-    def hidden_step(j, carry):
-        cols = columns(j)
+    def sweep(lo, hi, step, width=WIDTH):
+        count = (hi - lo) // width
+
+        def at_chunk(j, carry):
+            step(pl.multiple_of(lo + j * width, LANES), width)
+            return carry
+
+        if count > 1:
+            lax.fori_loop(0, count, at_chunk, 0)
+        elif count:
+            step(lo, width)
+        if lo + count * width < hi:
+            step(lo + count * width, hi - lo - count * width)
+
+    def hidden_step(start, width):
+        cols = pl.ds(start, width)
         gate = gate_ref[:, cols].astype(jnp.float32)
         sig = jax.nn.sigmoid(gate)
         hid[:, cols] = (gate * sig * up_ref[:, cols].astype(jnp.float32)).astype(jnp.bfloat16)
-        return carry
 
     for p, (lo, hi) in enumerate(sides):
-        lax.fori_loop(lo, hi, hidden_step, 0)
+        sweep(lo, hi, hidden_step, 2 * WIDTH)
         go(
             lambda p=p: (hid.at[:, halves[p]], hid_peer.at[:, halves[p]], core_recv.at[1 + p]),
             core_peer,
@@ -196,30 +219,26 @@
         ref = hid_peer.at[:, halves[p]]
         remote(ref, ref, send_sem.at[0], core_recv.at[1 + p], core_peer).wait_recv()
 
-    def grad_of(which, cols):
+    def grad_of(which, start, width):
+        cols = pl.ds(start, width)
         own = cot_rows_ref[core, which].reshape(outer * rows, tokens)
         other = cot_peer[which].reshape(outer * rows, tokens)
         value = jnp.dot(own, hid[:, cols], preferred_element_type=jnp.float32)
         value += jnp.dot(other, hid_peer[:, cols], preferred_element_type=jnp.float32)
         return value.reshape(outer, rows, width)
 
-    def send_step(j, carry):
-        cols = columns(j)
-        mid_send[:, :, cols] = grad_of(1 - mid, cols).astype(jnp.bfloat16)
-        return carry
-
-    def wide_columns(j):
-        return pl.ds(pl.multiple_of(j * width - early, width), width)
-
-    def wide_step(j, carry):
+    def send_step(start, width):
+        mid_send[:, :, pl.ds(start, width)] = grad_of(1 - mid, start, width).astype(jnp.bfloat16)
+
+    def own_step(start, width):
+        own_sum[:, :, pl.ds(start, width)] = grad_of(mid, start, width)
+
+    def wide_columns(start, width):
+        return pl.ds(pl.multiple_of(start - early, LANES), width)
+
+    def wide_step(start, width):
         for m in range(MID):
-            wide_sum[m, :, :, wide_columns(j)] = grad_of(m, columns(j))
-        return carry
-
-    def own_step(j, carry):
-        cols = columns(j)
-        own_sum[:, :, cols] = grad_of(mid, cols)
-        return carry
+            wide_sum[m, :, :, wide_columns(start, width)] = grad_of(m, start, width)
 
     def target(i):
         if i == last:
@@ -228,15 +247,12 @@
         down = jnp.where(down <= out, down - 1, down)
         return jnp.where(low, down, jnp.where(i >= out, i + 1, i))
 
-    def reduce_across(i):
+    def reduce_across(i, h):
         t = target(i)
-        for h in range(2):
-            go(
-                lambda h=h: (
-                    mid_send.at[t, :, pieces[h]], mid_recv.at[t, :, pieces[h]], mid_recv_sem.at[h, t],
-                ),
-                mid_peer,
-            )
+        go(
+            lambda: (mid_send.at[t, :, pieces[h]], mid_recv.at[t, :, pieces[h]], mid_recv_sem.at[h, t]),
+            mid_peer,
+        )
 
     def mid_wait(t, h):
         ref = mid_recv.at[t, :, pieces[h]]
@@ -254,13 +270,12 @@
         toward = {"dp": at(out + 1 - 2 * d, mid, core)}
 
         def step(chained):
-            def inner(j, carry):
-                cols = columns(j)
+            def inner(start, width):
+                cols = pl.ds(start, width)
                 value = own_sum[t, :, cols] + mid_recv[t, :, cols].astype(jnp.float32)
                 if chained:
                     value += line_recv[d, t, :, cols].astype(jnp.float32)
                 line_send[t, :, cols] = value.astype(jnp.bfloat16)
-                return carry
 
             return inner
 
@@ -270,11 +285,11 @@
             @pl.when(more)
             def _():
                 line_wait(d, t, h)
-                lax.fori_loop(lo, hi, step(True), 0)
+                sweep(lo, hi, step(True))
 
             @pl.when(jnp.logical_not(more))
             def _():
-                lax.fori_loop(lo, hi, step(False), 0)
+                sweep(lo, hi, step(False))
 
             go(
                 lambda: (
@@ -301,13 +316,12 @@
         toward = {"dp": at(out + 1 - 2 * d, mid, core)}
 
         def step(chained):
-            def inner(j, carry):
-                cols = wide_columns(j)
+            def inner(start, width):
+                cols = wide_columns(start, width)
                 value = wide_sum[m, t, :, cols]
                 if chained:
                     value += wide_recv[d, m, t, :, cols].astype(jnp.float32)
                 wide_send[m, t, :, cols] = value.astype(jnp.bfloat16)
-                return carry
 
             return inner
 
@@ -315,11 +329,11 @@
             @pl.when(more)
             def _():
                 wide_wait(d, m, t)
-                lax.fori_loop(first, chunks, step(True), 0)
+                sweep(early, ff, step(True))
 
             @pl.when(jnp.logical_not(more))
             def _():
-                lax.fori_loop(first, chunks, step(False), 0)
+                sweep(early, ff, step(False))
 
             go(
                 lambda: (wide_send.at[m, t], wide_recv.at[d, m, t], wide_recv_sem.at[d, m, t]),
@@ -343,12 +357,11 @@
     def wide_across():
         wide_arrived(1 - mid)
 
-        def step(j, carry):
-            cols = wide_columns(j)
+        def step(start, width):
+            cols = wide_columns(start, width)
             cross_send[:, cols] = wide_total(1 - mid, cols).astype(jnp.bfloat16)
-            return carry
-
-        lax.fori_loop(first, chunks, step, 0)
+
+        sweep(early, ff, step)
         go(lambda: (cross_send, cross_recv, cross_recv_sem), mid_peer)
 
     @pl.when(jnp.logical_not(has_prev))
@@ -388,8 +401,8 @@
         )
         cot = cot_ref[:, pl.ds(pl.multiple_of(g * deep, deep), deep)]
 
-        def step(i, carry):
-            cols = columns(i)
+        def step(start, width):
+            cols = pl.ds(start, width)
             grad = jnp.dot(
                 cot, weights[pl.ds(g * block, block), :, cols].reshape(deep, width),
                 preferred_element_type=jnp.float32,
@@ -404,109 +417,72 @@
                 sig = jax.nn.sigmoid(gate)
                 gate_grad_ref[:, cols] = (grad * up_val * sig * (1.0 + gate * (1.0 - sig))).astype(jnp.bfloat16)
                 up_grad_ref[:, cols] = (grad * gate * sig).astype(jnp.bfloat16)
-            return carry
-
-        lax.fori_loop(0, chunks, step, 0)
+
+        sweep(0, ff, step, ff if j < last else BROAD)
 
     edge = jnp.logical_or(out == 0, out == last)
     inner = jnp.logical_not(edge)
-    ref = cot_peer
-    remote(ref, ref, send_sem.at[0], core_recv.at[0], core_peer).wait_recv()
-    core_wait(0)
-    lax.fori_loop(first, chunks, wide_step, 0)
-    for p in range(MID):
-        wide_on(0, p, edge)
-    across_first()
-    along(1, mid, 0)
-    core_wait(1)
-    lax.fori_loop(0, first, send_step, 0)
-    reduce_across(0)
-    lax.fori_loop(0, first, own_step, 0)
-    along(1, mid, 1)
-    if last > 1:
-        for p in range(MID):
-            wide_on(1, p, edge)
-    across_last(0)
-    along(1, 1 - mid, 1)
-    use_block(0)
-    across_last(1)
-    wide_on(0, 0, inner)
-    pass_on(0, 0, edge)
-    if last > 1:
-        along(2, mid, 0)
-    reduce_across(1)
-    wide_on(0, 1, inner)
-    pass_on(0, 1, edge)
-    if last > 1:
-        use_block(1)
-    for k in range(2, outer):
-        along(k, mid, 1)
-        if k == 2:
-            wide_on(1, 0, inner)
-        along(k, 1 - mid, 1)
-        if k == 2:
-            wide_on(1, 1, inner)
-        if k < last:
-            for p in range(MID):
-                wide_on(k, p, edge)
-        if k == 2:
-            pass_on(0, 0, inner)
-        if k < last:
-            along(k + 1, mid, 0)
-            reduce_across(k)
-        if k == last - 1:
-            reduce_across(last)
-        if k == 2:
-            pass_on(0, 1, inner)
-        if k < last:
-            for p in range(MID):
-                wide_on(k, p, inner)
-        across_last(k)
-        if k < last:
-            pass_on(k - 1, 0, edge)
-            pass_on(k - 1, 1, edge)
-            use_block(k)
-    for h in range(2):
-        for k in range(last - 1, 0, -1):
-            pass_on(k, h, inner)
-    wide_across()
-    if last > 1:
-        pass_on(last - 1, 0, edge)
-        pass_on(last - 1, 1, edge)
-    use_block(last)
     loads[4].wait()
     loads[5].wait()
 
     def update_step(total_of):
-        def step(j, carry):
-            cols = columns(j)
+        def step(start, width):
+            cols = pl.ds(start, width)
             master_new, moment, square = adam(
-                total_of(j) / jnp.float32(total), master_ref[:, cols], one_ref[:, cols], two_ref[:, cols]
+                total_of(start, width) / jnp.float32(total),
+                master_ref[:, cols], one_ref[:, cols], two_ref[:, cols],
             )
             master_new_ref[:, cols] = master_new
             first_ref[:, cols] = moment
             second_ref[:, cols] = square
-            return carry
 
         return step
 
-    def early_total(j):
-        cols = columns(j)
+    def early_total(start, width):
+        cols = pl.ds(start, width)
         value = own_sum[out, :, cols] + mid_recv[out, :, cols].astype(jnp.float32)
         return value + line_recv[0, out, :, cols].astype(jnp.float32) + line_recv[1, out, :, cols].astype(jnp.float32)
 
-    def late_total(j):
-        cols = wide_columns(j)
+    def late_total(start, width):
+        cols = wide_columns(start, width)
         return wide_total(mid, cols) + cross_recv[:, cols].astype(jnp.float32)
 
-    for h, (lo, hi) in enumerate(bounds):
+    def own_done(h):
         pl.when(has_prev)(lambda: line_wait(0, out, h))
         pl.when(has_next)(lambda: line_wait(1, out, h))
         mid_wait(out, h)
-        lax.fori_loop(lo, hi, update_step(early_total), 0)
-    wide_arrived(mid)
-    remote(cross_recv, cross_recv, send_sem.at[0], cross_recv_sem, mid_peer).wait_recv()
-    lax.fori_loop(first, chunks, update_step(late_total), 0)
+        sweep(*bounds[h], update_step(early_total))
+
+    def wide_done():
+        wide_arrived(mid)
+        remote(cross_recv, cross_recv, send_sem.at[0], cross_recv_sem, mid_peer).wait_recv()
+        sweep(early, ff, update_step(late_total))
+
+    def core_ready(p):
+        if p == 0:
+            remote(cot_peer, cot_peer, send_sem.at[0], core_recv.at[0], core_peer).wait_recv()
+        core_wait(p)
+
+    acts = {
+        "core": core_ready,
+        "wide": lambda: sweep(early, ff, wide_step, BROAD),
+        "send": lambda: sweep(0, early, send_step, 2 * BROAD),
+        "own": lambda: sweep(0, early, own_step, 2 * BROAD),
+        "along": lambda k, other, which: along(k, 1 - mid if other else mid, which),
+        "first": across_first,
+        "last": across_last,
+        "across": reduce_across,
+        "edge": lambda i, h: pass_on(i, h, edge),
+        "inner": lambda i, h: pass_on(i, h, inner),
+        "wedge": lambda i, p: wide_on(i, p, edge),
+        "winner": lambda i, p: wide_on(i, p, inner),
+        "cross": wide_across,
+        "block": use_block,
+        "fin": own_done,
+        "finw": wide_done,
+    }
+    for name, *given in ORDER:
+        acts[name](*given)
 
     for place in range(half):
         ref = part_recv.at[place]
@@ -550,7 +526,7 @@
     outer = size // (MID * CORES)
     deep = MID * CORES * rows
     split = max(1, round(ff * ALONG / 128)) * 128
-    early = max(1, round(ff * ACROSS / WIDTH)) * WIDTH
+    early = max(1, round(ff * ACROSS / LANES)) * LANES
     cot = out_grad.reshape(tokens, depth)
     hbm = pl.BlockSpec(memory_space=pl.ANY)
     bf, f32 = jnp.bfloat16, jnp.float32
@@ -646,7 +622,8 @@
     size = mesh.shape["dp"]
 
     def on_device(gate_pre, up_pre, out_grad, master, moment_one, moment_two):
-        tall = master.shape[0] % 32 == 0 and master.shape[1] % WIDTH == 0 and size in (2 * MID * CORES, 4 * MID * CORES)
+        line = size == LINE * MID * CORES
+        tall = line and master.shape[0] % 32 == 0 and master.shape[1] % LANES == 0 and master.shape[1] >= 8 * LANES
         step = functools.partial(in_one_kernel, size) if tall else with_collectives
         return step(gate_pre, up_pre, out_grad, master, moment_one, moment_two)
 

time: 55.9 us -> 54.5 us (0.975)
  Pallas kernels: 55.1 us -> 53.7 us
    pallas_call x1, Pallas kernels: 52.7 us -> 51.3 us  [in_one_kernel(): pl.pallas_call(functools.partial(fused, outer, tokens * size, split, earl...]
where the time goes in v4:
time: 54.5 us; the launch traced here: 54.3 us
  Pallas kernels  53.7 us (99%)
  between operations  0.64 us (1%)
    pallas_call x1, Pallas kernels, in_one_kernel(): pl.pallas_call(functools.partial(fused, outer, tokens * size, split, earl...  51.3 us
    pallas_call x1, Pallas kernels, handed_on(): pl.pallas_call(body, out_shape=[jax.ShapeDtypeStruct(value.shape, value.d...  2.42 us

profile of v4, /device:TPU:0, one launch (start us, length us, event | category | flops | bytes accessed | tf_op | source)
XLA Modules:
  0.0 54.3 jit_solution(15965582580411913435)
XLA Ops:
  0.6 51.3 %shard_map.109 = (bf16[256,512]{1,0:T(8,128)(2,1)S(1)}, bf16[256,2816]{1,0:T(8,128)(2,1)S(1)}, bf16[256,2816]{1,0:T(8,128)(2,1)S(1)}, f32[64,2816]{1,0:T(8,128)S...) custom-call(bf16[256,2816]{1,0:T(8,128)(2,1)} %bitcast.6, bf16[256,2816]{1,0:T(8,128)(2,1)} %bitcast.7, ...), custom_call_target="tpu_custom_call" | custom-call | tf_op jit(solution)/shard_map/pallas_call | solution.py:534
  51.9 2.4 %shard_map.110 = (bf16[256,512]{1,0:T(8,128)(2,1)}, bf16[256,2816]{1,0:T(8,128)(2,1)}, bf16[256,2816]{1,0:T(8,128)(2,1)}, f32[64,2816]{1,0:T(8,128)}, f32[64,2816]{1,0:T(8,128)}, /*index=5*/f32[64,2816]{1,0:T(8,128)}) custom-call(bf16[256,512]{1,0:T(8,128)(2,1)S(1)} %get-tuple-element.18.refs_0_, bf16[256,2816]{1,0:T(8,128)(2,1)S(1)} %get-tuple-element.19.refs_1_, ...), custom_call_target="tpu_custom_call" | custom-call | tf_op jit(solution)/shard_map/pallas_call | solution.py:513

commit v5 on v4

--- a/solution.py
+++ b/solution.py
@@ -17,20 +17,20 @@
 LANES = 128
 WIDTH = 256
 BROAD = 1408
-ALONG = 0.591
-ACROSS = 0.591
-LEAD = 0.462
+ALONG = 0.636
+ACROSS = 0.545
+LEAD = 0.500
 ORDER = (
-    ("first",), ("core", 0), ("core", 1), ("along", 1, 0, 0), ("wide",), ("wedge", 0, 0), ("send",),
-    ("across", 1, 0), ("wedge", 0, 1), ("last", 0), ("across", 0, 0), ("block", 0), ("along", 1, 0, 1),
-    ("across", 0, 1), ("across", 1, 1), ("wedge", 1, 0), ("winner", 0, 0), ("wedge", 2, 0),
-    ("along", 1, 1, 1), ("own",), ("along", 2, 0, 0), ("edge", 0, 1), ("winner", 0, 1), ("edge", 1, 1),
-    ("winner", 2, 0), ("across", 2, 1), ("edge", 0, 0), ("last", 1), ("wedge", 1, 1), ("winner", 1, 0),
-    ("inner", 0, 1), ("across", 2, 0), ("along", 2, 0, 1), ("edge", 1, 0), ("block", 1), ("along", 2, 1, 1),
-    ("wedge", 2, 1), ("along", 3, 0, 0), ("across", 3, 1), ("inner", 1, 1), ("winner", 2, 1), ("last", 2),
-    ("inner", 0, 0), ("edge", 2, 1), ("cross",), ("block", 2), ("edge", 2, 0), ("across", 3, 0),
-    ("along", 3, 0, 1), ("along", 3, 1, 1), ("last", 3), ("winner", 1, 1), ("inner", 2, 1), ("block", 3),
-    ("inner", 2, 0), ("inner", 1, 0), ("fin", 1), ("finw",), ("fin", 0),
+    ("core", 0), ("core", 1), ("first",), ("send",), ("along", 1, 0, 0), ("wide",), ("across", 1, 1),
+    ("across", 0, 1), ("last", 0), ("wedge", 0, 0), ("along", 1, 0, 1), ("along", 1, 1, 1), ("wedge", 1, 0),
+    ("wedge", 2, 0), ("across", 0, 0), ("winner", 0, 0), ("wedge", 0, 1), ("along", 2, 0, 0), ("own",),
+    ("last", 1), ("across", 1, 0), ("across", 2, 1), ("edge", 0, 1), ("edge", 0, 0), ("along", 2, 1, 1),
+    ("edge", 1, 1), ("winner", 1, 0), ("across", 2, 0), ("wedge", 1, 1), ("winner", 2, 0), ("along", 3, 0, 0),
+    ("edge", 1, 0), ("winner", 0, 1), ("along", 2, 0, 1), ("block", 0), ("inner", 0, 1), ("block", 1),
+    ("inner", 0, 0), ("last", 2), ("across", 3, 1), ("block", 2), ("winner", 2, 1), ("inner", 1, 1),
+    ("inner", 2, 1), ("cross",), ("wedge", 2, 1), ("edge", 2, 1), ("across", 3, 0), ("along", 3, 1, 1),
+    ("last", 3), ("edge", 2, 0), ("winner", 1, 1), ("along", 3, 0, 1), ("inner", 2, 0), ("block", 3),
+    ("inner", 1, 0), ("finw",), ("fin", 1), ("fin", 0),
 )
 
 

time: 54.5 us -> 53.8 us (0.987)
  Pallas kernels: 53.7 us -> 53 us
    pallas_call x1, Pallas kernels: 51.3 us -> 50.5 us  [in_one_kernel(): pl.pallas_call(functools.partial(fused, outer, tokens * size, split, earl...]
where the time goes in v5:
time: 53.8 us; the launch traced here: 53.6 us
  Pallas kernels  53 us (99%)
  between operations  0.64 us (1%)
    pallas_call x1, Pallas kernels, in_one_kernel(): pl.pallas_call(functools.partial(fused, outer, tokens * size, split, earl...  50.5 us
    pallas_call x1, Pallas kernels, handed_on(): pl.pallas_call(body, out_shape=[jax.ShapeDtypeStruct(value.shape, value.d...  2.42 us

profile of v5, /device:TPU:0, one launch (start us, length us, event | category | flops | bytes accessed | tf_op | source)
XLA Modules:
  0.0 53.6 jit_solution(13983978812840547718)
XLA Ops:
  0.6 50.5 %shard_map.109 = (bf16[256,512]{1,0:T(8,128)(2,1)S(1)}, bf16[256,2816]{1,0:T(8,128)(2,1)S(1)}, bf16[256,2816]{1,0:T(8,128)(2,1)S(1)}, f32[64,2816]{1,0:T(8,128)S...) custom-call(bf16[256,2816]{1,0:T(8,128)(2,1)} %bitcast.6, bf16[256,2816]{1,0:T(8,128)(2,1)} %bitcast.7, ...), custom_call_target="tpu_custom_call" | custom-call | tf_op jit(solution)/shard_map/pallas_call | solution.py:534
  51.2 2.4 %shard_map.110 = (bf16[256,512]{1,0:T(8,128)(2,1)}, bf16[256,2816]{1,0:T(8,128)(2,1)}, bf16[256,2816]{1,0:T(8,128)(2,1)}, f32[64,2816]{1,0:T(8,128)}, f32[64,2816]{1,0:T(8,128)}, /*index=5*/f32[64,2816]{1,0:T(8,128)}) custom-call(bf16[256,512]{1,0:T(8,128)(2,1)S(1)} %get-tuple-element.18.refs_0_, bf16[256,2816]{1,0:T(8,128)(2,1)S(1)} %get-tuple-element.19.refs_1_, ...), custom_call_target="tpu_custom_call" | custom-call | tf_op jit(solution)/shard_map/pallas_call | solution.py:513

commit v6 on v5

--- a/solution.py
+++ b/solution.py
@@ -37,7 +37,7 @@
 def adam(main_grad, master, moment_one, moment_two):
     first = 0.9 * moment_one + 0.1 * main_grad
     second = 0.95 * moment_two + 0.05 * main_grad * main_grad
-    update = first / (1.0 - first_power) / (jnp.sqrt(second / (1.0 - second_power)) + 1e-08)
+    update = first * (1.0 / (1.0 - first_power)) / (jnp.sqrt(second * (1.0 / (1.0 - second_power))) + 1e-08)
     return master - 0.003 * (update + 0.1 * master), first, second
 
 
@@ -429,7 +429,7 @@
         def step(start, width):
             cols = pl.ds(start, width)
             master_new, moment, square = adam(
-                total_of(start, width) / jnp.float32(total),
+                total_of(start, width) * jnp.float32(1.0 / total),
                 master_ref[:, cols], one_ref[:, cols], two_ref[:, cols],
             )
             master_new_ref[:, cols] = master_new
@@ -481,20 +481,24 @@
         "fin": own_done,
         "finw": wide_done,
     }
-    for name, *given in ORDER:
+    def settle():
+        for place in range(half):
+            ref = part_recv.at[place]
+            remote(ref, ref, send_sem.at[0], part_recv_sem.at[place], rep_peer).wait_recv()
+            out_ref[:, place * deep : (place + 1) * deep] = (
+                part[rep * half + place] + part_recv[place].astype(jnp.float32)
+            ).astype(jnp.bfloat16)
+        for make, given in started:
+            if given:
+                pl.when(functools.reduce(jnp.logical_and, given))(lambda: make().wait_send())
+            else:
+                make().wait_send()
+
+    for name, *given in ORDER[:-1]:
         acts[name](*given)
-
-    for place in range(half):
-        ref = part_recv.at[place]
-        remote(ref, ref, send_sem.at[0], part_recv_sem.at[place], rep_peer).wait_recv()
-        out_ref[:, place * deep : (place + 1) * deep] = (
-            part[rep * half + place] + part_recv[place].astype(jnp.float32)
-        ).astype(jnp.bfloat16)
-    for make, given in started:
-        if given:
-            pl.when(functools.reduce(jnp.logical_and, given))(lambda: make().wait_send())
-        else:
-            make().wait_send()
+    settle()
+    for name, *given in ORDER[-1:]:
+        acts[name](*given)
 
 
 def handed_on(values):

time: 53.8 us -> 53.6 us (level)
  no operation moved by 1% of the time
where the time goes in v6:
time: 53.6 us; the launch traced here: 53.4 us
  Pallas kernels  52.8 us (99%)
  between operations  0.64 us (1%)
    pallas_call x1, Pallas kernels, in_one_kernel(): pl.pallas_call(functools.partial(fused, outer, tokens * size, split, earl...  50.4 us
    pallas_call x1, Pallas kernels, handed_on(): pl.pallas_call(body, out_shape=[jax.ShapeDtypeStruct(value.shape, value.d...  2.42 us

profile of v6, /device:TPU:0, one launch (start us, length us, event | category | flops | bytes accessed | tf_op | source)
XLA Modules:
  0.0 53.4 jit_solution(9421116998152155190)
XLA Ops:
  0.6 50.4 %shard_map.109 = (bf16[256,512]{1,0:T(8,128)(2,1)S(1)}, bf16[256,2816]{1,0:T(8,128)(2,1)S(1)}, bf16[256,2816]{1,0:T(8,128)(2,1)S(1)}, f32[64,2816]{1,0:T(8,128)S...) custom-call(bf16[256,2816]{1,0:T(8,128)(2,1)} %bitcast.6, bf16[256,2816]{1,0:T(8,128)(2,1)} %bitcast.7, ...), custom_call_target="tpu_custom_call" | custom-call | tf_op jit(solution)/shard_map/pallas_call | solution.py:538
  51.0 2.4 %shard_map.110 = (bf16[256,512]{1,0:T(8,128)(2,1)}, bf16[256,2816]{1,0:T(8,128)(2,1)}, bf16[256,2816]{1,0:T(8,128)(2,1)}, f32[64,2816]{1,0:T(8,128)}, f32[64,2816]{1,0:T(8,128)}, /*index=5*/f32[64,2816]{1,0:T(8,128)}) custom-call(bf16[256,512]{1,0:T(8,128)(2,1)S(1)} %get-tuple-element.18.refs_0_, bf16[256,2816]{1,0:T(8,128)(2,1)S(1)} %get-tuple-element.19.refs_1_, ...), custom_call_target="tpu_custom_call" | custom-call | tf_op jit(solution)/shard_map/pallas_call | solution.py:517

commit v7 on v6

--- a/solution.py
+++ b/solution.py
@@ -19,7 +19,7 @@
 BROAD = 1408
 ALONG = 0.636
 ACROSS = 0.545
-LEAD = 0.500
+LEAD = 0.333
 ORDER = (
     ("core", 0), ("core", 1), ("first",), ("send",), ("along", 1, 0, 0), ("wide",), ("across", 1, 1),
     ("across", 0, 1), ("last", 0), ("wedge", 0, 0), ("along", 1, 0, 1), ("along", 1, 1, 1), ("wedge", 1, 0),
@@ -451,12 +451,12 @@
         pl.when(has_prev)(lambda: line_wait(0, out, h))
         pl.when(has_next)(lambda: line_wait(1, out, h))
         mid_wait(out, h)
-        sweep(*bounds[h], update_step(early_total))
+        sweep(*bounds[h], update_step(early_total), 2 * WIDTH)
 
     def wide_done():
         wide_arrived(mid)
         remote(cross_recv, cross_recv, send_sem.at[0], cross_recv_sem, mid_peer).wait_recv()
-        sweep(early, ff, update_step(late_total))
+        sweep(early, ff, update_step(late_total), 2 * WIDTH)
 
     def core_ready(p):
         if p == 0:

time: 53.6 us -> 53.6 us (level)
  no operation moved by 1% of the time
where the time goes in v7:
time: 53.6 us; the launch traced here: 53.4 us
  Pallas kernels  52.8 us (99%)
  between operations  0.64 us (1%)
    pallas_call x1, Pallas kernels, in_one_kernel(): pl.pallas_call(functools.partial(fused, outer, tokens * size, split, earl...  50.4 us
    pallas_call x1, Pallas kernels, handed_on(): pl.pallas_call(body, out_shape=[jax.ShapeDtypeStruct(value.shape, value.d...  2.42 us

profile of v7, /device:TPU:0, one launch (start us, length us, event | category | flops | bytes accessed | tf_op | source)
XLA Modules:
  0.0 53.4 jit_solution(4979016145075131696)
XLA Ops:
  0.6 50.4 %shard_map.109 = (bf16[256,512]{1,0:T(8,128)(2,1)S(1)}, bf16[256,2816]{1,0:T(8,128)(2,1)S(1)}, bf16[256,2816]{1,0:T(8,128)(2,1)S(1)}, f32[64,2816]{1,0:T(8,128)S...) custom-call(bf16[256,2816]{1,0:T(8,128)(2,1)} %bitcast.6, bf16[256,2816]{1,0:T(8,128)(2,1)} %bitcast.7, ...), custom_call_target="tpu_custom_call" | custom-call | tf_op jit(solution)/shard_map/pallas_call | solution.py:538
  51.0 2.4 %shard_map.110 = (bf16[256,512]{1,0:T(8,128)(2,1)}, bf16[256,2816]{1,0:T(8,128)(2,1)}, bf16[256,2816]{1,0:T(8,128)(2,1)}, f32[64,2816]{1,0:T(8,128)}, f32[64,2816]{1,0:T(8,128)}, /*index=5*/f32[64,2816]{1,0:T(8,128)}) custom-call(bf16[256,512]{1,0:T(8,128)(2,1)S(1)} %get-tuple-element.18.refs_0_, bf16[256,2816]{1,0:T(8,128)(2,1)S(1)} %get-tuple-element.19.refs_1_, ...), custom_call_target="tpu_custom_call" | custom-call | tf_op jit(solution)/shard_map/pallas_call | solution.py:517
